TPU v7x, 128 devices: a whole 4x4x4 slice. The times are simulated.
128 devices in a mesh: gx: 8 (over x, y_hi), gy: 16 (over z, y_lo, core).
Axes of the slice: x: 4, y: 4 (y_hi: 2, y_lo: 2; y = y_hi * 2 + y_lo), z: 4, core: 2. Of those that a mesh axis runs over, the one named last changes fastest.
Arguments:
- u_wind: float32 [64, 128, 2048], P(None, 'gx', 'gy'), may hold values from -6 to 6
- v_wind: float32 [64, 128, 2048], P(None, 'gx', 'gy'), may hold values from -6 to 6
- w_wind: float32 [64, 128, 2048], P(None, 'gx', 'gy'), may hold values from -4 to 4
- pressure: float32 [64, 128, 2048], P(None, 'gx', 'gy'), may hold values from -6 to 6
- terrain_level: int32 [128, 2048], P('gx', 'gy'), may hold values from 0 to 8
- zone_width: int32 [4], replicated, may hold values from 5 to 16
- stiffness: float32 [64], replicated, may hold values from 0.25 to 2
- inflow_profile: float32 [2, 64], replicated, may hold values from -5 to 5
Outputs:
- u_final: float32 [64, 128, 2048], P(None, 'gx', 'gy')
- v_final: float32 [64, 128, 2048], P(None, 'gx', 'gy')
- w_final: float32 [64, 128, 2048], P(None, 'gx', 'gy')
- p_final: float32 [64, 128, 2048], P(None, 'gx', 'gy')
Inputs may be any that keep to these rules, and one draw needn't show every extreme that they name: `zone_width`: zone widths in columns.
All inputs are finite; a program needn't handle non-finite values.
Results may differ from a plain program's by a relative error of at most 0.0001.
Values sent between devices are 32-bit elements; how exact they have to be, the bound alone decides.
No kernel may reach another device: no remote copies, remote signals or barrier semaphores. Data moves between devices by JAX's collectives and lax.ppermute only.
A program may use at most 128 MiB of HBM per device.

v0:
```python
import jax
import jax.numpy as jnp
from jax import lax
from jax.experimental import pallas as pl
from jax.experimental.pallas import tpu as pltpu
from jax.sharding import PartitionSpec as P

SUB = 6
ADV = 0.3
H = 0.4
RELAX = 0.5
WET_FROM = 8
HALO = 8

f32 = jnp.float32


def vmem():
    return pl.BlockSpec(memory_space=pltpu.VMEM)


def smem():
    return pl.BlockSpec(memory_space=pltpu.SMEM)


def lanes(shape):
    return lax.broadcasted_iota(jnp.int32, shape, len(shape) - 1)


def pack_y_kernel(u, v, w, p, terrain, stiff, inflow, ylo, yhi, coef):
    nz = u.shape[0]
    groups = nz // 8
    lane = lanes((16, 128))
    for f, ref in enumerate((u, v, w, p)):

        def body(g, carry, f=f, ref=ref):
            low = jnp.zeros((16, 128), f32)
            high = jnp.zeros((16, 128), f32)
            for s in range(8):
                value = ref[g * 8 + s]
                here = (lane >= 16 * s) & (lane < 16 * s + 16)
                low = jnp.where(here, pltpu.roll(value, 16 * s, 1), low)
                high = jnp.where(here, pltpu.roll(value, (16 * s - 112) % 128, 1), high)
            ylo[f * groups + g] = low
            yhi[f * groups + g] = high
            return carry

        lax.fori_loop(0, groups, body, 0)
    solid = terrain[...].astype(f32)
    ylo[4 * groups] = solid
    yhi[4 * groups] = solid
    one = jnp.ones((8, 128), f32)
    above = jnp.zeros((8, 128), f32)
    ratio = jnp.zeros((8, 128), f32)
    for k in range(nz - 1, -1, -1):
        g = jnp.full((8, 128), stiff[k], f32)
        inverse = one / (one + g + above * (one - ratio))
        coef[0, k] = inverse
        coef[1, k] = above * inverse
        coef[2, k] = g * inverse
        coef[3, k] = g
        coef[4, k] = (H * H) * g
        coef[5, k] = jnp.full((8, 128), inflow[0, k], f32)
        coef[6, k] = jnp.full((8, 128), inflow[1, k], f32)
        ratio = g * inverse
        above = g


def pack_x_kernel(u, v, w, p, terrain, north, south, uw, ue, vw, ve, ww, we, pw, pe):
    nz = u.shape[0]
    groups = nz // 8
    lane = lanes((16, 128))
    for f, (ref, west, east) in enumerate(((u, uw, ue), (v, vw, ve), (w, ww, we), (p, pw, pe))):
        ninth = f in (0, 3)

        def body(g, carry, f=f, ref=ref, west=west, east=east, ninth=ninth):
            for s in range(8):
                k = g * 8 + s
                west[k] = ref[k, 0:8, :]
                east[k] = ref[k, 8:16, :]
                if ninth:
                    west[nz + groups + g, s : s + 1, :] = ref[k, 8:9, :]
                    east[nz + groups + g, s : s + 1, :] = ref[k, 7:8, :]
            corner = jnp.where(
                lane % 16 < 8,
                pltpu.roll(south[f * groups + g], 120, 1),
                pltpu.roll(north[f * groups + g], 8, 1),
            )
            west[nz + g] = corner[0:8]
            east[nz + g] = corner[8:16]
            return carry

        lax.fori_loop(0, groups, body, 0)
    solid = terrain[...].astype(f32)
    side = side_tile(lane, north[4 * groups], south[4 * groups])
    last = nz + 2 * groups
    uw[last] = solid[0:8]
    ue[last] = solid[8:16]
    uw[last + 1] = side[0:8]
    ue[last + 1] = side[8:16]


def side_tile(lane, north, south):
    return jnp.where(lane < 16, north, jnp.where(lane >= 112, south, 0.0))


def extend(ref, f, north, south, west, east, g, s, ninth):
    nz = ref.shape[0]
    groups = nz // 8
    k = g * 8 + s
    lane16 = lanes((16, 128))
    lane8 = lanes((8, 128))
    own = side_tile(
        lane16,
        pltpu.roll(north[f * groups + g], (-16 * s) % 128, 1),
        pltpu.roll(south[f * groups + g], (112 - 16 * s) % 128, 1),
    )
    edge = (lane8 < 8) | (lane8 >= 120)
    back = (120 - 16 * s) % 128
    corner_west = jnp.where(edge, pltpu.roll(west[nz + g], back, 1), 0.0)
    corner_east = jnp.where(edge, pltpu.roll(east[nz + g], back, 1), 0.0)
    zero = jnp.zeros((8, 128), f32)
    extra = zero
    if ninth:
        row = lax.broadcasted_iota(jnp.int32, (8, 128), 0)
        far_east = jnp.broadcast_to(east[nz + groups + g, s : s + 1, :], (8, 128))
        far_west = jnp.broadcast_to(west[nz + groups + g, s : s + 1, :], (8, 128))
        extra = jnp.where(row == 0, far_east, jnp.where(row == 7, far_west, 0.0))
    main = jnp.concatenate([west[k], ref[k], east[k], extra], axis=0)
    side = jnp.concatenate([corner_west, own, corner_east, zero], axis=0)
    return jnp.concatenate([main, side], axis=1)


def face_difference(value, speed, dim):
    size = value.shape[dim]

    def at(by):
        return pltpu.roll(value, (-by) % size, dim)

    before, after = at(-1), at(1)
    before2, after2 = at(-2), at(2)
    before3 = at(-3)
    centred = 37.0 * (value + before) - 8.0 * (after + before2) + (after2 + before3)
    upwind = 10.0 * (value - before) - 5.0 * (after - before2) + (after2 - before3)
    flux = speed * centred - jnp.abs(speed) * upwind
    return pltpu.roll(flux, size - 1, dim) - flux


def advected(value, u, v):
    scale = ADV / 60.0
    across = face_difference(value, scale * u, 0)[0:32]
    along = face_difference(value[0:32], scale * v[0:32], 1)
    return value[0:32] - (across + along)


def advect_uv_kernel(
    u, v, terrain, zones, north, south, uw, ue, vw, ve, xu, xv, au, av, masks, damp
):
    nz = u.shape[0]
    groups = nz // 8
    lane = lanes((16, 128))
    own_side = side_tile(lane, north[4 * groups], south[4 * groups])
    last = nz + 2 * groups
    solid = jnp.concatenate(
        [
            jnp.concatenate([uw[last], terrain[...].astype(f32), ue[last]], axis=0),
            jnp.concatenate([uw[last + 1], own_side, ue[last + 1]], axis=0),
        ],
        axis=1,
    )
    shape = (32, 256)
    block_x, block_y = u.shape[1], u.shape[2]
    total_x = block_x * lax.axis_size("gx")
    total_y = block_y * lax.axis_size("gy")
    row = lax.broadcasted_iota(jnp.int32, shape, 0) - HALO
    col = lanes(shape)
    col = jnp.where(col < 192, col, col - 256)
    at_x = lax.axis_index("gx") * block_x + row
    at_y = lax.axis_index("gy") * block_y + col
    inside = (at_x >= 0) & (at_x < total_x) & (at_y >= 0) & (at_y < total_y)
    inside = inside & (col < block_y + 16) & (col >= -16)
    inside = jnp.where(inside, 1.0, 0.0).astype(f32)
    for k in range(WET_FROM):
        masks[k] = jnp.where(solid <= float(k), inside, 0.0)
    masks[WET_FROM] = inside
    at_x = at_x.astype(f32)
    at_y = at_y.astype(f32)
    ramp = jnp.zeros(shape, f32)
    for b, distance in enumerate((at_x, (total_x - 1.0) - at_x, at_y, (total_y - 1.0) - at_y)):
        width = jnp.full(shape, zones[b], jnp.int32).astype(f32)
        ramp = jnp.maximum(ramp, jnp.maximum(width - distance, 0.0) / width)
    relax = RELAX * ramp
    damp[0] = jnp.where(inside > 0.0, 1.0 - relax, 0.0)
    damp[1] = jnp.where(inside > 0.0, relax, 0.0)

    def fill(g, carry):
        for s in range(8):
            k = g * 8 + s
            xu[k] = extend(u, 0, north, south, uw, ue, g, s, True)
            xv[k] = extend(v, 1, north, south, vw, ve, g, s, False)
        return carry

    lax.fori_loop(0, groups, fill, 0)

    def level(k, carry):
        mask = masks[jnp.minimum(k, WET_FROM)]
        au[k] = mask * advected(xu[k], xu[k], xv[k])
        av[k] = mask * advected(xv[k], xu[k], xv[k])
        return carry

    lax.fori_loop(0, nz, level, 0)


def advect_one_kernel(x, xu, xv, masks, north, south, west, east, out, *, f):
    nz = x.shape[0]
    groups = nz // 8

    def body(g, carry):
        for s in range(8):
            k = g * 8 + s
            mask = H * masks[jnp.minimum(k, WET_FROM)]
            value = extend(x, f, north, south, west, east, g, s, f == 3)
            out[k] = mask * advected(value, xu[k], xv[k])
        return carry

    lax.fori_loop(0, groups, body, 0)


def splat(tile):
    tall = jnp.concatenate([tile] * 4, axis=0)
    return jnp.concatenate([tall, tall], axis=1)


def substeps_kernel(
    au, av, aw, ap, masks, damp, coef, uo, vo, wo, po, us, vs, ws, ps, qs, ds
):
    nz = au.shape[0]
    zero = jnp.zeros((32, 256), f32)

    for step in range(SUB):
        first, final = step == 0, step == SUB - 1
        ur, vr, wr, pr = (au, av, aw, ap) if first else (us, vs, ws, ps)

        def down(k, carry, masked):
            q_above, d_above = carry
            p = pr[k]
            mask = masks[k] if masked else masks[WET_FROM]
            u = mask * (ur[k] - (p - pltpu.roll(p, 1, 0)))
            v = mask * (vr[k] - (p - pltpu.roll(p, 1, 1)))
            divergence = (pltpu.roll(u, 31, 0) - u) + (pltpu.roll(v, 255, 1) - v)
            q = p - splat(coef[4, k]) * divergence
            d = (wr[k] - (q_above - q)) * splat(coef[0, k]) + splat(coef[1, k]) * d_above
            keep, pull = damp[0], damp[1]
            if masked:
                d = mask * d
                pull = mask * pull
            u = keep * u + pull * splat(coef[5, k])
            v = keep * v + pull * splat(coef[6, k])
            if final:
                uo[k] = u[8:24, 0:128]
                vo[k] = v[8:24, 0:128]
            else:
                us[k] = u
                vs[k] = v
            qs[k] = q
            ds[k] = d
            return q, d

        carry = lax.fori_loop(
            0, nz - WET_FROM, lambda t, c: down(nz - 1 - t, c, False), (zero, zero)
        )
        lax.fori_loop(0, WET_FROM, lambda t, c: down(WET_FROM - 1 - t, c, True), carry)

        def up(k, below, masked):
            w = ds[k] + splat(coef[2, k]) * below
            p = qs[k] - splat(coef[3, k]) * (w - below)
            keep = damp[0]
            if masked:
                p = masks[k] * p
            if final:
                wo[k] = ((1.0 / H) * (keep * w))[8:24, 0:128]
                po[k] = ((1.0 / H) * (keep * p))[8:24, 0:128]
            else:
                ws[k] = keep * w
                ps[k] = keep * p
            return w

        below = lax.fori_loop(0, WET_FROM, lambda k, c: up(k, c, True), zero)
        lax.fori_loop(WET_FROM, nz, lambda k, c: up(k, c, False), below)


def neighbours(axis, by):
    size = lax.axis_size(axis)
    return [(i, i + by) for i in range(size) if 0 <= i + by < size]


def on_device(u, v, w, p, terrain, zones, stiff, inflow):
    nz = u.shape[0]
    groups = nz // 8
    big = pltpu.CompilerParams(vmem_limit_bytes=60 * 1024 * 1024)

    def arr(*shape):
        return jax.ShapeDtypeStruct(shape, f32)

    ylo, yhi, coef = pl.pallas_call(
        pack_y_kernel,
        out_shape=(arr(4 * groups + 1, 16, 128), arr(4 * groups + 1, 16, 128), arr(7, nz, 8, 128)),
        in_specs=[vmem()] * 5 + [smem()] * 2,
        out_specs=(vmem(),) * 3,
        compiler_params=big,
        name="pack_y",
    )(u, v, w, p, terrain, stiff, inflow)
    north = lax.ppermute(ylo, "gy", neighbours("gy", -1))
    south = lax.ppermute(yhi, "gy", neighbours("gy", 1))
    tiles_of = (nz + 2 * groups + 2, nz + groups, nz + groups, nz + 2 * groups)
    sent = pl.pallas_call(
        pack_x_kernel,
        out_shape=tuple(arr(t, 8, 128) for t in tiles_of for _ in range(2)),
        in_specs=[vmem()] * 7,
        out_specs=(vmem(),) * 8,
        compiler_params=big,
        name="pack_x",
    )(u, v, w, p, terrain, north, south)
    east = [lax.ppermute(m, "gx", neighbours("gx", -1)) for m in sent[0::2]]
    west = [lax.ppermute(m, "gx", neighbours("gx", 1)) for m in sent[1::2]]
    xu, xv, au, av, masks, damp = pl.pallas_call(
        advect_uv_kernel,
        out_shape=(
            arr(nz, 40, 256),
            arr(nz, 40, 256),
            arr(nz, 32, 256),
            arr(nz, 32, 256),
            arr(WET_FROM + 1, 32, 256),
            arr(2, 32, 256),
        ),
        in_specs=[vmem()] * 3 + [smem()] + [vmem()] * 6,
        out_specs=(vmem(),) * 6,
        compiler_params=big,
        name="advect_uv",
    )(u, v, terrain, zones, north, south, west[0], east[0], west[1], east[1])

    def advect_one(x, f):
        def kernel(*refs):
            advect_one_kernel(*refs, f=f)

        return pl.pallas_call(
            kernel,
            out_shape=arr(nz, 32, 256),
            in_specs=[vmem()] * 8,
            out_specs=vmem(),
            compiler_params=big,
            name="advect_w" if f == 2 else "advect_p",
        )(x, xu, xv, masks, north, south, west[f], east[f])

    aw = advect_one(w, 2)
    ap = advect_one(p, 3)
    out = arr(nz, 16, 128)
    return pl.pallas_call(
        substeps_kernel,
        out_shape=(out,) * 4,
        in_specs=[vmem()] * 7,
        out_specs=(vmem(),) * 4,
        scratch_shapes=[pltpu.VMEM((nz, 32, 256), f32)] * 6,
        compiler_params=big,
        name="substeps",
    )(au, av, aw, ap, masks, damp, coef)


def solution(mesh):
    field = P(None, "gx", "gy")
    return jax.shard_map(
        on_device,
        mesh=mesh,
        in_specs=(field, field, field, field, P("gx", "gy"), P(), P(), P()),
        out_specs=(field, field, field, field),
        check_vma=False,
    )
```

profile of v0, /device:TPU:110, one launch (start us, length us, event | category | flops | bytes accessed | tf_op | source)
XLA Modules:
  0.0 202.4 jit_solution(10732774668444697267)
XLA Ops:
  0.6 6.5 %pack_y.1 = (f32[33,16,128]{2,1,0:T(8,128)}, f32[33,16,128]{2,1,0:T(8,128)}, f32[7,64,8,128]{3,2,1,0:T(8,128)}) custom-call(f32[64,16,128]{2,1,0:T(8,128)} %u.5, f32[64,16,128]{2,1,0:T(8,128)} %v.5, f32[64,16,128]{2,1,0:T(8,128)} %refs_0_.2, f32[64,16,128]{2,1,0:T(8,128)} %refs_0_.3, s32[16,128]{1,0:T(8,128)} %terrain.5, f32[64]{0:T(128)} %stiff.1, ...), custom_call_target="tpu_custom_call" | custom-call | tf_op jit(solution)/shard_map/pack_y/pallas_call | solution.py:305
  7.1 1.9 collective-permute-start
  9.0 2.4 %collective-permute-start.1 = (f32[33,16,128]{2,1,0:T(8,128)}, f32[33,16,128]{2,1,0:T(8,128)S(1)}, u32[]{:S(2)}, u32[]{:S(2)}) collective-permute-start(f32[33,16,128]{2,1,0:T(8,128)} %get-tuple-element.22), channel_id=1, source_target_pairs={{0,1},{1,2},{2,3},{3,4},{4,5},{5,6},{6,7},{7,8},{8,9},{9,10},{10,1... | collective-permute-start | bytes 811016 | tf_op jit(solution)/shard_map/ppermute | solution.py:314
  11.5 1.8 collective-permute-done.north.refs_4_
  13.3 4.5 %collective-permute-done.1.south.refs_5_ = f32[33,16,128]{2,1,0:T(8,128)S(1)} collective-permute-done((f32[33,16,128]{2,1,0:T(8,128)}, f32[33,16,128]{2,1,0:T(8,128)S(1)}, u32[]{:S(2)}, u32[]{:S(2)}) %collective-permute-start.1) | collective-permute-done | bytes 270368 | tf_op jit(solution)/shard_map/ppermute | solution.py:314
  17.8 0.7 copy-done.1
  18.5 5.5 %pack_x.1 = (f32[82,8,128]{2,1,0:T(8,128)}, f32[82,8,128]{2,1,0:T(8,128)}, f32[72,8,128]{2,1,0:T(8,128)}, f32[72,8,128]{2,1,0:T(8,128)}, f32[72,8,128]{2,1,0:T(8...) custom-call(f32[64,16,128]{2,1,0:T(8,128)} %u.5, f32[64,16,128]{2,1,0:T(8,128)} %v.5, ...), custom_call_target="tpu_custom_call" | custom-call | tf_op jit(solution)/shard_map/pack_x/pallas_call | solution.py:316
  24.1 4.2 %collective-permute-start.2 = (f32[82,8,128]{2,1,0:T(8,128)}, f32[82,8,128]{2,1,0:T(8,128)S(1)}, u32[]{:S(2)}, u32[]{:S(2)}) collective-permute-start(f32[82,8,128]{2,1,0:T(8,128)} %get-tuple-element.23), channel_id=1, source_target_pairs={{0,16},{16,32},{32,48},{48,64},{64,80},{80,96},{96,112},{1,17},{17... | collective-permute-start | bytes 1007624 | tf_op jit(solution)/shard_map/ppermute | solution.py:325
  28.3 1.9 collective-permute-start.4
  30.2 6.3 %collective-permute-start.5 = (f32[72,8,128]{2,1,0:T(8,128)}, f32[72,8,128]{2,1,0:T(8,128)S(1)}, u32[]{:S(2)}, u32[]{:S(2)}) collective-permute-start(f32[72,8,128]{2,1,0:T(8,128)} %get-tuple-element.26), channel_id=1, source_target_pairs={{16,0},{32,16},{48,32},{64,48},{80,64},{96,80},{112,96},{17,1},{33... | collective-permute-start | bytes 884744 | tf_op jit(solution)/shard_map/ppermute | solution.py:324
  36.5 3.1 %collective-permute-start.3 = (f32[82,8,128]{2,1,0:T(8,128)}, f32[82,8,128]{2,1,0:T(8,128)S(1)}, u32[]{:S(2)}, u32[]{:S(2)}) collective-permute-start(f32[82,8,128]{2,1,0:T(8,128)} %get-tuple-element.24), channel_id=1, source_target_pairs={{16,0},{32,16},{48,32},{64,48},{80,64},{96,80},{112,96},{17,1},{33... | collective-permute-start | bytes 1007624 | tf_op jit(solution)/shard_map/ppermute | solution.py:324
  39.7 4.2 %collective-permute-start.8 = (f32[80,8,128]{2,1,0:T(8,128)}, f32[80,8,128]{2,1,0:T(8,128)S(1)}, u32[]{:S(2)}, u32[]{:S(2)}) collective-permute-start(f32[80,8,128]{2,1,0:T(8,128)} %get-tuple-element.34), channel_id=1, source_target_pairs={{0,16},{16,32},{32,48},{48,64},{64,80},{80,96},{96,112},{1,17},{17... | collective-permute-start | bytes 983048 | tf_op jit(solution)/shard_map/ppermute | solution.py:325
  43.9 21.8 %collective-permute-start.9 = (f32[80,8,128]{2,1,0:T(8,128)}, f32[80,8,128]{2,1,0:T(8,128)S(1)}, u32[]{:S(2)}, u32[]{:S(2)}) collective-permute-start(f32[80,8,128]{2,1,0:T(8,128)} %get-tuple-element.35), channel_id=1, source_target_pairs={{16,0},{32,16},{48,32},{64,48},{80,64},{96,80},{112,96},{17,1},{33... | collective-permute-start | bytes 983048 | tf_op jit(solution)/shard_map/ppermute | solution.py:324
  65.7 0.0 collective-permute-done.5.ve
  65.7 1.9 collective-permute-start.6
  67.7 0.0 collective-permute-done.2.uw
  67.7 0.0 copy-start.2
  67.7 6.3 %collective-permute-start.7 = (f32[72,8,128]{2,1,0:T(8,128)}, f32[72,8,128]{2,1,0:T(8,128)S(1)}, u32[]{:S(2)}, u32[]{:S(2)}) collective-permute-start(f32[72,8,128]{2,1,0:T(8,128)} %get-tuple-element.33), channel_id=1, source_target_pairs={{16,0},{32,16},{48,32},{64,48},{80,64},{96,80},{112,96},{17,1},{33... | collective-permute-start | bytes 884744 | tf_op jit(solution)/shard_map/ppermute | solution.py:324
  74.1 0.0 copy-start.3
  74.1 0.7 copy-done.3
  74.8 23.6 %advect_uv.1 = (f32[64,40,256]{2,1,0:T(8,128)}, f32[64,40,256]{2,1,0:T(8,128)}, f32[64,32,256]{2,1,0:T(8,128)}, f32[64,32,256]{2,1,0:T(8,128)}, f32[9,32,256]{2,1,0:T(8,128)}, /*index=5*/f32[2,32,256]{2,1,0:T(8,128)}) custom-call(f32[64,16,128]{2,1,0:T(8,128)} %u.5, f32[64,16,128]{2,1,0:T(8,128)} %v.5, s32[16,128]{1,0:T(8,128)} %terrain.5, s32[4]{0:T(128)} %zones.1, ...), custom_call_target="tpu_custom_call" | custom-call | tf_op jit(solution)/shard_map/advect_uv/pallas_call | solution.py:326
  98.4 0.0 collective-permute-done.8.refs_6_
  98.4 0.0 copy-start.4
  98.5 0.0 copy-start.5
  98.5 0.7 copy-done.4
  99.2 0.1 copy-done.5
  99.3 14.2 %advect_p.1.ap = f32[64,32,256]{2,1,0:T(8,128)} custom-call(f32[64,16,128]{2,1,0:T(8,128)} %refs_0_.3, f32[64,40,256]{2,1,0:T(8,128)} %get-tuple-element.29.refs_1_, f32[64,40,256]{2,1,0:T(8,128)} %get-tuple-element.30.refs_2_, f32[9,32,256]{2,1,0:T(8,128)} %get-tuple-element.31.refs_3_.masks, f32[33,16,128]{2,1,0:T(8,128)} %copy-done, ...), custom_call_target="tpu_custom_call" | custom-call | tf_op jit(solution)/shard_map/advect_p/pallas_call | solution.py:346
  113.5 0.0 collective-permute-done.6.refs_6_
  113.5 0.7 copy-done.8
  114.2 0.7 copy-done.9
  114.9 14.3 %advect_w.1.aw = f32[64,32,256]{2,1,0:T(8,128)} custom-call(f32[64,16,128]{2,1,0:T(8,128)} %refs_0_.2, f32[64,40,256]{2,1,0:T(8,128)} %get-tuple-element.29.refs_1_, f32[64,40,256]{2,1,0:T(8,128)} %get-tuple-element.30.refs_2_, f32[9,32,256]{2,1,0:T(8,128)} %get-tuple-element.31.refs_3_.masks, f32[33,16,128]{2,1,0:T(8,128)} %copy-done, ...), custom_call_target="tpu_custom_call" | custom-call | tf_op jit(solution)/shard_map/advect_w/pallas_call | solution.py:346
  129.2 73.2 %substeps.1 = (f32[64,16,128]{2,1,0:T(8,128)}, f32[64,16,128]{2,1,0:T(8,128)}, f32[64,16,128]{2,1,0:T(8,128)}, f32[64,16,128]{2,1,0:T(8,128)}) custom-call(f32[64,32,256]{2,1,0:T(8,128)} %get-tuple-element.27.au, f32[64,32,256]{2,1,0:T(8,128)} %get-tuple-element.28.av, f32[64,32,256]{2,1,0:T(8,128)} %advect_w.1.aw, f32[64,32,256]{2,1,0:T(8,128)} %advect_p.1.ap, ...), custom_call_target="tpu_custom_call" | custom-call | tf_op jit(solution)/shard_map/substeps/pallas_call | solution.py:358
  (14 shorter events, 0.0 us)
Async XLA Ops:
  7.1 6.2 %collective-permute-start = (f32[33,16,128]{2,1,0:T(8,128)}, f32[33,16,128]{2,1,0:T(8,128)S(1)}, u32[]{:S(2)}, u32[]{:S(2)}) collective-permute-start(f32[33,16,128]{2,1,0:T(8,128)} %get-tuple-element.21), channel_id=1, source_target_pairs={{1,0},{2,1},{3,2},{4,3},{5,4},{6,5},{7,6},{8,7},{9,8},{10,9},{11,1... | collective-permute-start | bytes 811016 | tf_op jit(solution)/shard_map/ppermute | solution.py:313
  9.0 8.8 %collective-permute-start.1 = (f32[33,16,128]{2,1,0:T(8,128)}, f32[33,16,128]{2,1,0:T(8,128)S(1)}, u32[]{:S(2)}, u32[]{:S(2)}) collective-permute-start(f32[33,16,128]{2,1,0:T(8,128)} %get-tuple-element.22), channel_id=1, source_target_pairs={{0,1},{1,2},{2,3},{3,4},{4,5},{5,6},{6,7},{7,8},{8,9},{9,10},{10,1... | collective-permute-start | bytes 811016 | tf_op jit(solution)/shard_map/ppermute | solution.py:314
  13.3 4.5 %copy-start = (f32[33,16,128]{2,1,0:T(8,128)}, f32[33,16,128]{2,1,0:T(8,128)S(1)}, u32[]{:S(2)}) copy-start(f32[33,16,128]{2,1,0:T(8,128)S(1)} %collective-permute-done.north.refs_4_) | copy-start | bytes 811012
  17.8 0.7 copy-start.1
  24.1 43.6 %collective-permute-start.2 = (f32[82,8,128]{2,1,0:T(8,128)}, f32[82,8,128]{2,1,0:T(8,128)S(1)}, u32[]{:S(2)}, u32[]{:S(2)}) collective-permute-start(f32[82,8,128]{2,1,0:T(8,128)} %get-tuple-element.23), channel_id=1, source_target_pairs={{0,16},{16,32},{32,48},{48,64},{64,80},{80,96},{96,112},{1,17},{17... | collective-permute-start | bytes 1007624 | tf_op jit(solution)/shard_map/ppermute | solution.py:325
  28.3 15.6 %collective-permute-start.4 = (f32[72,8,128]{2,1,0:T(8,128)}, f32[72,8,128]{2,1,0:T(8,128)S(1)}, u32[]{:S(2)}, u32[]{:S(2)}) collective-permute-start(f32[72,8,128]{2,1,0:T(8,128)} %get-tuple-element.25), channel_id=1, source_target_pairs={{0,16},{16,32},{32,48},{48,64},{64,80},{80,96},{96,112},{1,17},{17... | collective-permute-start | bytes 884744 | tf_op jit(solution)/shard_map/ppermute | solution.py:325
  30.2 35.5 %collective-permute-start.5 = (f32[72,8,128]{2,1,0:T(8,128)}, f32[72,8,128]{2,1,0:T(8,128)S(1)}, u32[]{:S(2)}, u32[]{:S(2)}) collective-permute-start(f32[72,8,128]{2,1,0:T(8,128)} %get-tuple-element.26), channel_id=1, source_target_pairs={{16,0},{32,16},{48,32},{64,48},{80,64},{96,80},{112,96},{17,1},{33... | collective-permute-start | bytes 884744 | tf_op jit(solution)/shard_map/ppermute | solution.py:324
  36.5 37.5 %collective-permute-start.3 = (f32[82,8,128]{2,1,0:T(8,128)}, f32[82,8,128]{2,1,0:T(8,128)S(1)}, u32[]{:S(2)}, u32[]{:S(2)}) collective-permute-start(f32[82,8,128]{2,1,0:T(8,128)} %get-tuple-element.24), channel_id=1, source_target_pairs={{16,0},{32,16},{48,32},{64,48},{80,64},{96,80},{112,96},{17,1},{33... | collective-permute-start | bytes 1007624 | tf_op jit(solution)/shard_map/ppermute | solution.py:324
  39.7 58.7 %collective-permute-start.8 = (f32[80,8,128]{2,1,0:T(8,128)}, f32[80,8,128]{2,1,0:T(8,128)S(1)}, u32[]{:S(2)}, u32[]{:S(2)}) collective-permute-start(f32[80,8,128]{2,1,0:T(8,128)} %get-tuple-element.34), channel_id=1, source_target_pairs={{0,16},{16,32},{32,48},{48,64},{64,80},{80,96},{96,112},{1,17},{17... | collective-permute-start | bytes 983048 | tf_op jit(solution)/shard_map/ppermute | solution.py:325
  43.9 30.1 %copy-start.6 = (f32[72,8,128]{2,1,0:T(8,128)}, f32[72,8,128]{2,1,0:T(8,128)S(1)}, u32[]{:S(2)}) copy-start(f32[72,8,128]{2,1,0:T(8,128)S(1)} %collective-permute-done.4.vw) | copy-start | bytes 884740
  43.9 54.5 %collective-permute-start.9 = (f32[80,8,128]{2,1,0:T(8,128)}, f32[80,8,128]{2,1,0:T(8,128)S(1)}, u32[]{:S(2)}, u32[]{:S(2)}) collective-permute-start(f32[80,8,128]{2,1,0:T(8,128)} %get-tuple-element.35), channel_id=1, source_target_pairs={{16,0},{32,16},{48,32},{64,48},{80,64},{96,80},{112,96},{17,1},{33... | collective-permute-start | bytes 983048 | tf_op jit(solution)/shard_map/ppermute | solution.py:324
  65.7 8.3 %copy-start.7 = (f32[72,8,128]{2,1,0:T(8,128)}, f32[72,8,128]{2,1,0:T(8,128)S(1)}, u32[]{:S(2)}) copy-start(f32[72,8,128]{2,1,0:T(8,128)S(1)} %collective-permute-done.5.ve) | copy-start | bytes 884740
  65.7 47.7 %collective-permute-start.6 = (f32[72,8,128]{2,1,0:T(8,128)}, f32[72,8,128]{2,1,0:T(8,128)S(1)}, u32[]{:S(2)}, u32[]{:S(2)}) collective-permute-start(f32[72,8,128]{2,1,0:T(8,128)} %get-tuple-element.32), channel_id=1, source_target_pairs={{0,16},{16,32},{32,48},{48,64},{64,80},{80,96},{96,112},{1,17},{17... | collective-permute-start | bytes 884744 | tf_op jit(solution)/shard_map/ppermute | solution.py:325
  67.7 6.4 %copy-start.2 = (f32[82,8,128]{2,1,0:T(8,128)}, f32[82,8,128]{2,1,0:T(8,128)S(1)}, u32[]{:S(2)}) copy-start(f32[82,8,128]{2,1,0:T(8,128)S(1)} %collective-permute-done.2.uw) | copy-start | bytes 1007620
  67.7 45.8 %collective-permute-start.7 = (f32[72,8,128]{2,1,0:T(8,128)}, f32[72,8,128]{2,1,0:T(8,128)S(1)}, u32[]{:S(2)}, u32[]{:S(2)}) collective-permute-start(f32[72,8,128]{2,1,0:T(8,128)} %get-tuple-element.33), channel_id=1, source_target_pairs={{16,0},{32,16},{48,32},{64,48},{80,64},{96,80},{112,96},{17,1},{33... | collective-permute-start | bytes 884744 | tf_op jit(solution)/shard_map/ppermute | solution.py:324
  74.1 0.7 copy-start.3
  98.4 0.7 copy-start.4
  98.5 0.8 copy-start.5
  113.5 0.7 copy-start.8
  114.2 0.7 copy-start.9
where the time goes:
time: 203 us; the launch traced here: 202 us
  Pallas kernels  137 us (67%)
  starting transfers between devices  54.1 us (27%)
  waiting for transfers between devices  6.4 us (3%)
  local copies, waits for them, and re-layouts  3.67 us (2%)
    pallas_call x1, Pallas kernels, on_device(): pl.pallas_call(substeps_kernel, out_shape=(out,) * 4, in_specs=[vmem()] *...  73.2 us
    ppermute x4, starting transfers between devices, on_device(): east = [lax.ppermute(m, 'gx', neighbours('gx', -1)) for m in sent[0::2]]  37.6 us
    pallas_call x2, Pallas kernels, advect_one(): pl.pallas_call(kernel, out_shape=arr(nz, 32, 256), in_specs=[vmem()] * 8,...  28.5 us
    pallas_call x1, Pallas kernels, on_device(): pl.pallas_call(advect_uv_kernel, out_shape=(arr(nz, 40, 256), arr(nz, 40,...  23.6 us
    ppermute x4, starting transfers between devices, on_device(): west = [lax.ppermute(m, 'gx', neighbours('gx', 1)) for m in sent[1::2]]  12.3 us
    pallas_call x1, Pallas kernels, on_device(): pl.pallas_call(pack_y_kernel, out_shape=(arr(4 * groups + 1, 16, 128), ar...  6.48 us
    pallas_call x1, Pallas kernels, on_device(): pl.pallas_call(pack_x_kernel, out_shape=tuple((arr(t, 8, 128) for t in ti...  5.53 us
    ppermute x1, waiting for transfers between devices, on_device(): south = lax.ppermute(yhi, 'gy', neighbours('gy', 1))  4.54 us
  transfers between devices with their start and end apart: 10, of which 2 were waited for; matrix products, arithmetic and copies ran while one was open for 0% of the time, Pallas kernels for 19%

commit v1 on v0

v1 whole, which is shorter than its diff:
```python
import jax
import jax.numpy as jnp
import numpy as np
from jax import lax
from jax.experimental import pallas as pl
from jax.experimental.pallas import tpu as pltpu
from jax.sharding import PartitionSpec as P

SUB = 6
ADV = 0.3
H = 0.4
RELAX = 0.5
WET_FROM = 8
HALO = 8

f32 = jnp.float32
UD, UU = 8, 8


def vmem():
    return pl.BlockSpec(memory_space=pltpu.VMEM)


def smem():
    return pl.BlockSpec(memory_space=pltpu.SMEM)


def lanes(shape):
    return lax.broadcasted_iota(jnp.int32, shape, len(shape) - 1)


def pack_a_kernel(u, v, w, p, terrain, ylo, yhi, west, east):
    nz = u.shape[0]
    groups = nz // 8
    lane = lanes((16, 128))
    for f, ref in enumerate((u, v, w, p)):

        def body(g, carry, f=f, ref=ref):
            rolled = []
            for s in range(8):
                k = g * 8 + s
                value = ref[k]
                rolled.append(pltpu.roll(value, 16 * s, 1))
                if f < 2:
                    west[f * nz + k] = value[0:8]
                    east[f * nz + k] = value[8:16]
            low = rolled[0]
            high = rolled[0]
            for s in range(1, 8):
                low = jnp.where(lane // 16 == s, rolled[s], low)
                high = jnp.where(lane // 16 == s - 1, rolled[s], high)
            ylo[f * groups + g] = low
            yhi[f * groups + g] = high
            return carry

        lax.fori_loop(0, groups, body, 0, unroll=2)
    solid = terrain[...].astype(f32)
    ylo[4 * groups] = solid
    yhi[4 * groups] = solid


def pack_b_kernel(w, p, stiff, inflow, north, ww, we, pw, pe, coef):
    nz = w.shape[0]
    for ref, west, east in ((w, ww, we), (p, pw, pe)):
        west[...] = ref[:, 0:8, :]
        east[...] = ref[:, 8:16, :]
    one = jnp.ones((8, 128), f32)
    above = jnp.zeros((8, 128), f32)
    ratio = jnp.zeros((8, 128), f32)
    for k in range(nz - 1, -1, -1):
        g = jnp.full((8, 128), stiff[k], f32)
        inverse = one / (one + g + above * (one - ratio))
        coef[0, k] = inverse
        coef[1, k] = above * inverse
        coef[2, k] = g * inverse
        coef[3, k] = g
        coef[4, k] = (H * H) * g
        coef[5, k] = jnp.full((8, 128), inflow[0, k], f32)
        coef[6, k] = jnp.full((8, 128), inflow[1, k], f32)
        ratio = g * inverse
        above = g


def pack_c_kernel(u, p, terrain, north, south, cw, ce):
    nz = u.shape[0]
    groups = nz // 8
    lane = lanes((16, 128))
    for t in range(4 * groups):
        corner = jnp.where(lane % 16 < 8, north[t], south[t])
        cw[t] = corner[0:8]
        ce[t] = corner[8:16]
    for f, ref in enumerate((u, p)):

        def body(g, carry, f=f, ref=ref):
            for s in range(8):
                cw[(4 + f) * groups + g, s : s + 1, :] = ref[g * 8 + s, 8:9, :]
                ce[(4 + f) * groups + g, s : s + 1, :] = ref[g * 8 + s, 7:8, :]
            return carry

        lax.fori_loop(0, groups, body, 0)
    solid = terrain[...].astype(f32)
    side = side_tile(lane, north[4 * groups], south[4 * groups])
    last = 6 * groups
    cw[last] = solid[0:8]
    ce[last] = solid[8:16]
    cw[last + 1] = side[0:8]
    ce[last + 1] = side[8:16]


def side_tile(lane, north, south):
    return jnp.where(lane < 16, north, jnp.where(lane >= 112, south, 0.0))


def extend(ref, f, north, south, west, east, far_w, far_e, g, s, base=0):
    groups = ref.shape[0] // 8
    k = g * 8 + s
    lane16 = lanes((16, 128))
    lane8 = lanes((8, 128))
    back = (-16 * s) % 128
    t = f * groups + g
    own = side_tile(lane16, pltpu.roll(north[t], back, 1), pltpu.roll(south[t], back, 1))
    edge = (lane8 < 8) | (lane8 >= 120)
    corner_west = jnp.where(edge, pltpu.roll(far_w[t], back, 1), 0.0)
    corner_east = jnp.where(edge, pltpu.roll(far_e[t], back, 1), 0.0)
    zero = jnp.zeros((8, 128), f32)
    extra = zero
    if f in (0, 3):
        t = (4 if f == 0 else 5) * groups + g
        row = lax.broadcasted_iota(jnp.int32, (8, 128), 0)
        ninth_e = jnp.broadcast_to(far_e[t, s : s + 1, :], (8, 128))
        ninth_w = jnp.broadcast_to(far_w[t, s : s + 1, :], (8, 128))
        extra = jnp.where(row == 0, ninth_e, jnp.where(row == 7, ninth_w, 0.0))
    main = jnp.concatenate([west[base + k], ref[k], east[base + k], extra], axis=0)
    side = jnp.concatenate([corner_west, own, corner_east, zero], axis=0)
    return jnp.concatenate([main, side], axis=1)


BAND = ((0, 37, 10), (-1, 37, -10), (1, -8, -5), (-2, -8, 5), (2, 1, 1), (-3, 1, -1))


def band_matrix():
    band = np.zeros((256, 512), np.float32)
    j = np.arange(256)
    for by, centred, upwind in BAND:
        band[(j + by) % 256, j] = centred
        band[(j + by) % 256, 256 + j] = upwind
    return jnp.asarray(band, jnp.bfloat16)


def stage(parts, s, value):
    rows = slice(32 * s, 32 * s + 32)
    for part in parts:
        piece = value.astype(jnp.bfloat16)
        part[rows, :] = piece
        value = value - piece.astype(f32)


def along_sums(parts, band, sums):
    total = jnp.dot(parts[0][...], band[...], preferred_element_type=f32)
    for part in parts[1:]:
        total = total + jnp.dot(part[...], band[...], preferred_element_type=f32)
    sums[...] = total


def advected(value, u, v, sums, s):
    scale = ADV / 60.0

    def at(by):
        return pltpu.roll(value, (-by) % 40, 0)

    before, after = at(-1), at(1)
    before2, after2 = at(-2), at(2)
    before3 = at(-3)
    centred = 37.0 * (value + before) - 8.0 * (after + before2) + (after2 + before3)
    upwind = 10.0 * (value - before) - 5.0 * (after - before2) + (after2 - before3)
    speed = scale * u
    flux = speed * centred - jnp.abs(speed) * upwind
    across = (pltpu.roll(flux, 39, 0) - flux)[0:32]
    rows = slice(32 * s, 32 * s + 32)
    speed = scale * v[0:32]
    flux = speed * sums[rows, 0:256] - jnp.abs(speed) * sums[rows, 256:512]
    along = pltpu.roll(flux, 255, 1) - flux
    return value[0:32] - (across + along)


def advect_uv_kernel(
    u,
    v,
    terrain,
    zones,
    north,
    south,
    cw,
    ce,
    west,
    east,
    band,
    xu,
    xv,
    au,
    av,
    masks,
    damp,
    *scratch,
):
    parts, sums = scratch[0:3], scratch[3]
    nz = u.shape[0]
    groups = nz // 8
    lane = lanes((16, 128))
    own_side = side_tile(lane, north[4 * groups], south[4 * groups])
    last = 6 * groups
    solid = jnp.concatenate(
        [
            jnp.concatenate([cw[last], terrain[...].astype(f32), ce[last]], axis=0),
            jnp.concatenate([cw[last + 1], own_side, ce[last + 1]], axis=0),
        ],
        axis=1,
    )
    shape = (32, 256)
    block_x, block_y = u.shape[1], u.shape[2]
    total_x = block_x * lax.axis_size("gx")
    total_y = block_y * lax.axis_size("gy")
    row = lax.broadcasted_iota(jnp.int32, shape, 0) - HALO
    col = lanes(shape)
    col = jnp.where(col < 192, col, col - 256)
    at_x = lax.axis_index("gx") * block_x + row
    at_y = lax.axis_index("gy") * block_y + col
    inside = (at_x >= 0) & (at_x < total_x) & (at_y >= 0) & (at_y < total_y)
    inside = inside & (col < block_y + 16) & (col >= -16)
    inside = jnp.where(inside, 1.0, 0.0).astype(f32)
    for k in range(WET_FROM):
        masks[k] = jnp.where(solid <= float(k), inside, 0.0)
    masks[WET_FROM] = inside
    at_x = at_x.astype(f32)
    at_y = at_y.astype(f32)
    ramp = jnp.zeros(shape, f32)
    for b, distance in enumerate((at_x, (total_x - 1.0) - at_x, at_y, (total_y - 1.0) - at_y)):
        width = jnp.full(shape, zones[b], jnp.int32).astype(f32)
        ramp = jnp.maximum(ramp, jnp.maximum(width - distance, 0.0) / width)
    relax = RELAX * ramp
    damp[0] = jnp.where(inside > 0.0, 1.0 - relax, 0.0)
    damp[1] = jnp.where(inside > 0.0, relax, 0.0)

    def body(g, carry):
        for s in range(8):
            k = g * 8 + s
            xu[k] = extend(u, 0, north, south, west, east, cw, ce, g, s)
            xv[k] = extend(v, 1, north, south, west, east, cw, ce, g, s, nz)
        for x, out in ((xu, au), (xv, av)):
            for s in range(8):
                stage(parts, s, x[g * 8 + s, 0:32, :])
            along_sums(parts, band, sums)
            for s in range(8):
                k = g * 8 + s
                mask = masks[jnp.minimum(k, WET_FROM)]
                out[k] = mask * advected(x[k], xu[k], xv[k], sums, s)
        return carry

    lax.fori_loop(0, groups, body, 0)


def advect_one_kernel(
    x, xu, xv, masks, north, south, cw, ce, west, east, band, out, *scratch, f
):
    parts, sums, values = scratch[0:3], scratch[3], scratch[4]
    nz = x.shape[0]
    groups = nz // 8

    def body(g, carry):
        for s in range(8):
            value = extend(x, f, north, south, west, east, cw, ce, g, s)
            values[s] = value
            stage(parts, s, value[0:32])
        along_sums(parts, band, sums)
        for s in range(8):
            k = g * 8 + s
            mask = H * masks[jnp.minimum(k, WET_FROM)]
            out[k] = mask * advected(values[s], xu[k], xv[k], sums, s)
        return carry

    lax.fori_loop(0, groups, body, 0)


def advect_scratch():
    part = pltpu.VMEM((256, 256), jnp.bfloat16)
    return [part, part, part, pltpu.VMEM((256, 512), f32)]


def splat(tile):
    tall = jnp.concatenate([tile] * 4, axis=0)
    return jnp.concatenate([tall, tall], axis=1)


def substeps_kernel(
    au, av, aw, ap, masks, damp, coef, uo, vo, wo, po, us, vs, ws, ps, qs, ds
):
    nz = au.shape[0]
    zero = jnp.zeros((32, 256), f32)

    for step in range(SUB):
        first, final = step == 0, step == SUB - 1
        ur, vr, wr, pr = (au, av, aw, ap) if first else (us, vs, ws, ps)

        def down(k, carry, masked):
            q_above, d_above = carry
            p = pr[k]
            mask = masks[k] if masked else masks[WET_FROM]
            u = mask * (ur[k] - (p - pltpu.roll(p, 1, 0)))
            v = mask * (vr[k] - (p - pltpu.roll(p, 1, 1)))
            divergence = (pltpu.roll(u, 31, 0) - u) + (pltpu.roll(v, 255, 1) - v)
            q = p - splat(coef[4, k]) * divergence
            d = (wr[k] - (q_above - q)) * splat(coef[0, k]) + splat(coef[1, k]) * d_above
            keep, pull = damp[0], damp[1]
            if masked:
                d = mask * d
                pull = mask * pull
            u = keep * u + pull * splat(coef[5, k])
            v = keep * v + pull * splat(coef[6, k])
            if final:
                uo[k] = u[8:24, 0:128]
                vo[k] = v[8:24, 0:128]
            else:
                us[k] = u
                vs[k] = v
            qs[k] = q
            ds[k] = d
            return q, d

        carry = lax.fori_loop(
            0, nz - WET_FROM, lambda t, c: down(nz - 1 - t, c, False), (zero, zero), unroll=UD
        )
        lax.fori_loop(0, WET_FROM, lambda t, c: down(WET_FROM - 1 - t, c, True), carry, unroll=UD)

        def up(k, below, masked):
            w = ds[k] + splat(coef[2, k]) * below
            p = qs[k] - splat(coef[3, k]) * (w - below)
            keep = damp[0]
            if masked:
                p = masks[k] * p
            if final:
                wo[k] = ((1.0 / H) * (keep * w))[8:24, 0:128]
                po[k] = ((1.0 / H) * (keep * p))[8:24, 0:128]
            else:
                ws[k] = keep * w
                ps[k] = keep * p
            return w

        below = lax.fori_loop(0, WET_FROM, lambda k, c: up(k, c, True), zero, unroll=UU)
        lax.fori_loop(WET_FROM, nz, lambda k, c: up(k, c, False), below, unroll=UU)


def neighbours(axis, by):
    size = lax.axis_size(axis)
    return [(i, i + by) for i in range(size) if 0 <= i + by < size]


def send(value, axis, by):
    return lax.ppermute(value, axis, neighbours(axis, by))


def on_device(u, v, w, p, terrain, zones, stiff, inflow):
    nz = u.shape[0]
    groups = nz // 8

    def room(mib):
        return pltpu.CompilerParams(vmem_limit_bytes=mib * 1024 * 1024)


    def arr(*shape):
        return jax.ShapeDtypeStruct(shape, f32)

    slab = arr(nz, 8, 128)
    ylo, yhi, uw, ue = pl.pallas_call(
        pack_a_kernel,
        out_shape=(arr(4 * groups + 1, 16, 128),) * 2 + (arr(2 * nz, 8, 128),) * 2,
        in_specs=[vmem()] * 5,
        out_specs=(vmem(),) * 4,
        compiler_params=room(6),
        name="pack_a",
    )(u, v, w, p, terrain)
    north = send(ylo, "gy", -1)
    south = send(yhi, "gy", 1)
    ue_in, uw_in = send(uw, "gx", -1), send(ue, "gx", 1)
    cw, ce = pl.pallas_call(
        pack_c_kernel,
        out_shape=(arr(6 * groups + 2, 8, 128),) * 2,
        in_specs=[vmem()] * 5,
        out_specs=(vmem(),) * 2,
        compiler_params=room(4),
        name="pack_c",
    )(u, p, terrain, north, south)
    ce_in, cw_in = send(cw, "gx", -1), send(ce, "gx", 1)
    ww, we, pw, pe, coef = pl.pallas_call(
        pack_b_kernel,
        out_shape=(slab,) * 4 + (arr(7, nz, 8, 128),),
        in_specs=[vmem()] * 2 + [smem()] * 2 + [pl.BlockSpec(memory_space=pl.ANY)],
        out_specs=(vmem(),) * 5,
        compiler_params=room(6),
        name="pack_b",
    )(w, p, stiff, inflow, north)
    we_in, ww_in = send(ww, "gx", -1), send(we, "gx", 1)
    pe_in, pw_in = send(pw, "gx", -1), send(pe, "gx", 1)
    band = band_matrix()
    advect_uv = pl.pallas_call(
        advect_uv_kernel,
        out_shape=(
            arr(nz, 40, 256),
            arr(nz, 40, 256),
            arr(nz, 32, 256),
            arr(nz, 32, 256),
            arr(WET_FROM + 1, 32, 256),
            arr(2, 32, 256),
        ),
        in_specs=[vmem()] * 3 + [smem()] + [vmem()] * 7,
        out_specs=(vmem(),) * 6,
        scratch_shapes=advect_scratch(),
        compiler_params=room(18),
        name="advect_uv",
    )
    xu, xv, au, av, masks, damp = advect_uv(
        u, v, terrain, zones, north, south, cw_in, ce_in, uw_in, ue_in, band
    )

    def advect_one(x, f, west, east):
        def kernel(*refs):
            advect_one_kernel(*refs, f=f)

        return pl.pallas_call(
            kernel,
            out_shape=arr(nz, 32, 256),
            in_specs=[vmem()] * 11,
            out_specs=vmem(),
            scratch_shapes=advect_scratch() + [pltpu.VMEM((8, 40, 256), f32)],
            compiler_params=room(14),
            name="advect_w" if f == 2 else "advect_p",
        )(x, xu, xv, masks, north, south, cw_in, ce_in, west, east, band)

    aw = advect_one(w, 2, ww_in, we_in)
    ap = advect_one(p, 3, pw_in, pe_in)
    out = arr(nz, 16, 128)
    return pl.pallas_call(
        substeps_kernel,
        out_shape=(out,) * 4,
        in_specs=[vmem()] * 7,
        out_specs=(vmem(),) * 4,
        scratch_shapes=[pltpu.VMEM((nz, 32, 256), f32)] * 6,
        compiler_params=room(28),
        name="substeps",
    )(au, av, aw, ap, masks, damp, coef)


def solution(mesh):
    field = P(None, "gx", "gy")
    return jax.shard_map(
        on_device,
        mesh=mesh,
        in_specs=(field, field, field, field, P("gx", "gy"), P(), P(), P()),
        out_specs=(field, field, field, field),
        check_vma=False,
    )
```

time: 203 us -> 114 us (0.56)
  the two profiles are of different devices: /device:TPU:110 before, /device:TPU:99 now
where the time goes in v1:
time: 114 us
  Pallas kernels  43.1 us (38%)
  starting transfers between devices  37.3 us (33%)
  waiting for transfers between devices  27.3 us (24%)
  local copies, waits for them, and re-layouts  4.89 us (4%)
    ppermute x10, starting transfers between devices, send(): return lax.ppermute(value, axis, neighbours(axis, by))  37.3 us
    ppermute x10, waiting for transfers between devices, send(): return lax.ppermute(value, axis, neighbours(axis, by))  27.3 us
    pallas_call x1, Pallas kernels, on_device(): pl.pallas_call(substeps_kernel, out_shape=(out,) * 4, in_specs=[vmem()] *...  19.3 us
    pallas_call x2, Pallas kernels, advect_one(): pl.pallas_call(kernel, out_shape=arr(nz, 32, 256), in_specs=[vmem()] * 11...  10.6 us
    pallas_call x1, Pallas kernels, on_device(): advect_uv(u, v, terrain, zones, north, south, cw_in, ce_in, uw_in, ue_in,...  10.2 us
    unnamed x28, local copies, waits for them, and re-layouts  4.89 us
  transfers between devices with their start and end apart: 10, of which 2 were waited for; matrix products, arithmetic and copies ran while one was open for 0% of the time, Pallas kernels for 15%

profile of v1, /device:TPU:99, one launch (start us, length us, event | category | flops | bytes accessed | tf_op | source)
XLA Modules:
  0.0 113.6 jit_solution(9634546578503894295)
XLA Ops:
  0.6 1.0 copy-done
  1.7 1.0 copy-done.2
  2.7 1.0 copy-done.4
  3.8 1.0 copy-done.7
  4.8 0.7 copy-done.9
  5.5 0.0 copy-start.6
  5.6 1.6 %pack_a.1 = (f32[33,16,128]{2,1,0:T(8,128)S(1)}, f32[33,16,128]{2,1,0:T(8,128)S(1)}, f32[128,8,128]{2,1,0:T(8,128)S(1)}, f32[128,8,128]{2,1,0:T(8,128)S(1)}) custom-call(f32[64,16,128]{2,1,0:T(8,128)S(1)} %copy-done.4, f32[64,16,128]{2,1,0:T(8,128)S(1)} %copy-done.7, f32[64,16,128]{2,1,0:T(8,128)S(1)} %copy-done.2, f32[64,16,128]{2,1,0:T(8,128)S(1)} %copy-done, ...), custom_call_target="tpu_custom_call" | custom-call | tf_op jit(solution)/shard_map/pack_a/pallas_call | solution.py:373
  7.1 4.8 %collective-permute-start.4 = (f32[128,8,128]{2,1,0:T(8,128)S(1)}, f32[128,8,128]{2,1,0:T(8,128)S(1)}, u32[]{:S(2)}, u32[]{:S(2)}) collective-permute-start(f32[128,8,128]{2,1,0:T(8,128)S(1)} %get-tuple-element.25), channel_id=1, source_target_pairs={{0,16},{16,32},{32,48},{48,64},{64,80},{80,96},{96,112},{1,17},{17... | collective-permute-start | bytes 1572872 | tf_op jit(solution)/shard_map/ppermute | solution.py:358
  12.0 2.9 %collective-permute-start = (f32[33,16,128]{2,1,0:T(8,128)S(1)}, f32[33,16,128]{2,1,0:T(8,128)S(1)}, u32[]{:S(2)}, u32[]{:S(2)}) collective-permute-start(f32[33,16,128]{2,1,0:T(8,128)S(1)} %get-tuple-element.21), channel_id=1, source_target_pairs={{1,0},{2,1},{3,2},{4,3},{5,4},{6,5},{7,6},{8,7},{9,8},{10,9},{11,1... | collective-permute-start | bytes 811016 | tf_op jit(solution)/shard_map/ppermute | solution.py:358
  14.8 2.7 %collective-permute-start.1 = (f32[33,16,128]{2,1,0:T(8,128)S(1)}, f32[33,16,128]{2,1,0:T(8,128)S(1)}, u32[]{:S(2)}, u32[]{:S(2)}) collective-permute-start(f32[33,16,128]{2,1,0:T(8,128)S(1)} %get-tuple-element.22), channel_id=1, source_target_pairs={{0,1},{1,2},{2,3},{3,4},{4,5},{5,6},{6,7},{7,8},{8,9},{9,10},{10,1... | collective-permute-start | bytes 811016 | tf_op jit(solution)/shard_map/ppermute | solution.py:358
  17.5 3.9 %collective-permute-start.5 = (f32[128,8,128]{2,1,0:T(8,128)S(1)}, f32[128,8,128]{2,1,0:T(8,128)S(1)}, u32[]{:S(2)}, u32[]{:S(2)}) collective-permute-start(f32[128,8,128]{2,1,0:T(8,128)S(1)} %get-tuple-element.26), channel_id=1, source_target_pairs={{16,0},{32,16},{48,32},{64,48},{80,64},{96,80},{112,96},{17,1},{33... | collective-permute-start | bytes 1572872 | tf_op jit(solution)/shard_map/ppermute | solution.py:358
  21.4 23.5 %collective-permute-done.north.refs_4_ = f32[33,16,128]{2,1,0:T(8,128)S(1)} collective-permute-done((f32[33,16,128]{2,1,0:T(8,128)S(1)}, f32[33,16,128]{2,1,0:T(8,128)S(1)}, u32[]{:S(2)}, u32[]{:S(2)}) %collective-permute-start) | collective-permute-done | bytes 270368 | tf_op jit(solution)/shard_map/ppermute | solution.py:358
  44.9 0.0 collective-permute-done.1.south.refs_5_
  44.9 0.2 pack_c.1
  45.1 1.9 %collective-permute-start.2 = (f32[50,8,128]{2,1,0:T(8,128)S(1)}, f32[50,8,128]{2,1,0:T(8,128)S(1)}, u32[]{:S(2)}, u32[]{:S(2)}) collective-permute-start(f32[50,8,128]{2,1,0:T(8,128)S(1)} %get-tuple-element.23), channel_id=1, source_target_pairs={{0,16},{16,32},{32,48},{48,64},{64,80},{80,96},{96,112},{1,17},{17... | collective-permute-start | bytes 614408 | tf_op jit(solution)/shard_map/ppermute | solution.py:358
  47.0 5.8 %collective-permute-start.3 = (f32[50,8,128]{2,1,0:T(8,128)S(1)}, f32[50,8,128]{2,1,0:T(8,128)S(1)}, u32[]{:S(2)}, u32[]{:S(2)}) collective-permute-start(f32[50,8,128]{2,1,0:T(8,128)S(1)} %get-tuple-element.24), channel_id=1, source_target_pairs={{16,0},{32,16},{48,32},{64,48},{80,64},{96,80},{112,96},{17,1},{33... | collective-permute-start | bytes 614408 | tf_op jit(solution)/shard_map/ppermute | solution.py:358
  52.8 1.2 %pack_b.1 = (f32[64,8,128]{2,1,0:T(8,128)S(1)}, f32[64,8,128]{2,1,0:T(8,128)S(1)}, f32[64,8,128]{2,1,0:T(8,128)S(1)}, f32[64,8,128]{2,1,0:T(8,128)S(1)}, f32[7,64,8,128]{3,2,1,0:T(8,128)S(1)}) custom-call(f32[64,16,128]{2,1,0:T(8,128)S(1)} %copy-done.3, f32[64,16,128]{2,1,0:T(8,128)S(1)} %copy-done.1, f32[64]{0:T(128)S(1)} %copy-done.12, ...), custom_call_target="tpu_custom_call" | custom-call | tf_op jit(solution)/shard_map/pack_b/pallas_call | solution.py:393
  54.1 4.1 %collective-permute-start.8 = (f32[64,8,128]{2,1,0:T(8,128)S(1)}, f32[64,8,128]{2,1,0:T(8,128)S(1)}, u32[]{:S(2)}, u32[]{:S(2)}) collective-permute-start(f32[64,8,128]{2,1,0:T(8,128)S(1)} %get-tuple-element.34), channel_id=1, source_target_pairs={{0,16},{16,32},{32,48},{48,64},{64,80},{80,96},{96,112},{1,17},{17... | collective-permute-start | bytes 786440 | tf_op jit(solution)/shard_map/ppermute | solution.py:358
  58.2 0.0 collective-permute-done.2.cw.refs_6_
  58.2 3.5 %collective-permute-start.9 = (f32[64,8,128]{2,1,0:T(8,128)S(1)}, f32[64,8,128]{2,1,0:T(8,128)S(1)}, u32[]{:S(2)}, u32[]{:S(2)}) collective-permute-start(f32[64,8,128]{2,1,0:T(8,128)S(1)} %get-tuple-element.35), channel_id=1, source_target_pairs={{16,0},{32,16},{48,32},{64,48},{80,64},{96,80},{112,96},{17,1},{33... | collective-permute-start | bytes 786440 | tf_op jit(solution)/shard_map/ppermute | solution.py:358
  61.8 3.9 %collective-permute-done.3.ce.refs_7_ = f32[50,8,128]{2,1,0:T(8,128)S(1)} collective-permute-done((f32[50,8,128]{2,1,0:T(8,128)S(1)}, f32[50,8,128]{2,1,0:T(8,128)S(1)}, u32[]{:S(2)}, u32[]{:S(2)}) %collective-permute-start.3) | collective-permute-done | bytes 204832 | tf_op jit(solution)/shard_map/ppermute | solution.py:358
  65.6 1.9 %collective-permute-start.6 = (f32[64,8,128]{2,1,0:T(8,128)S(1)}, f32[64,8,128]{2,1,0:T(8,128)S(1)}, u32[]{:S(2)}, u32[]{:S(2)}) collective-permute-start(f32[64,8,128]{2,1,0:T(8,128)S(1)} %get-tuple-element.32), channel_id=1, source_target_pairs={{0,16},{16,32},{32,48},{48,64},{64,80},{80,96},{96,112},{1,17},{17... | collective-permute-start | bytes 786440 | tf_op jit(solution)/shard_map/ppermute | solution.py:358
  67.6 0.0 collective-permute-done.4.west
  67.6 5.8 %collective-permute-start.7 = (f32[64,8,128]{2,1,0:T(8,128)S(1)}, f32[64,8,128]{2,1,0:T(8,128)S(1)}, u32[]{:S(2)}, u32[]{:S(2)}) collective-permute-start(f32[64,8,128]{2,1,0:T(8,128)S(1)} %get-tuple-element.33), channel_id=1, source_target_pairs={{16,0},{32,16},{48,32},{64,48},{80,64},{96,80},{112,96},{17,1},{33... | collective-permute-start | bytes 786440 | tf_op jit(solution)/shard_map/ppermute | solution.py:358
  73.3 0.0 collective-permute-done.5.east
  73.4 10.2 %advect_uv.1 = (f32[64,40,256]{2,1,0:T(8,128)S(1)}, f32[64,40,256]{2,1,0:T(8,128)S(1)}, f32[64,32,256]{2,1,0:T(8,128)S(1)}, f32[64,32,256]{2,1,0:T(8,128)S(1)}, ...) custom-call(f32[64,16,128]{2,1,0:T(8,128)S(1)} %copy-done.5, f32[64,16,128]{2,1,0:T(8,128)S(1)} %copy-done.8, ...), custom_call_target="tpu_custom_call" | custom-call | tf_op jit(solution)/shard_map/advect_uv/pallas_call | solution.py:420
  83.6 0.0 collective-permute-done.8.refs_8_
  83.6 0.0 collective-permute-done.9.refs_9_
  83.6 5.4 %advect_p.1.ap = f32[64,32,256]{2,1,0:T(8,128)S(1)} custom-call(f32[64,16,128]{2,1,0:T(8,128)S(1)} %copy-done.1, f32[64,40,256]{2,1,0:T(8,128)S(1)} %get-tuple-element.29.refs_1_, f32[64,40,256]{2,1,0:T(8,128)S(1)} %get-tuple-element.30.refs_2_, f32[9,32,256]{2,1,0:T(8,128)S(1)} %get-tuple-element.31.refs_3_.masks, ...), custom_call_target="tpu_custom_call" | custom-call | tf_op jit(solution)/shard_map/advect_p/pallas_call | solution.py:428
  89.0 0.0 collective-permute-done.6.refs_8_
  89.0 5.3 %advect_w.1.aw = f32[64,32,256]{2,1,0:T(8,128)S(1)} custom-call(f32[64,16,128]{2,1,0:T(8,128)S(1)} %copy-done.3, f32[64,40,256]{2,1,0:T(8,128)S(1)} %get-tuple-element.29.refs_1_, f32[64,40,256]{2,1,0:T(8,128)S(1)} %get-tuple-element.30.refs_2_, f32[9,32,256]{2,1,0:T(8,128)S(1)} %get-tuple-element.31.refs_3_.masks, ...), custom_call_target="tpu_custom_call" | custom-call | tf_op jit(solution)/shard_map/advect_w/pallas_call | solution.py:428
  94.3 19.3 %substeps.1 = (f32[64,16,128]{2,1,0:T(8,128)}, f32[64,16,128]{2,1,0:T(8,128)}, f32[64,16,128]{2,1,0:T(8,128)}, f32[64,16,128]{2,1,0:T(8,128)}) custom-call(f32[64,32,256]{2,1,0:T(8,128)S(1)} %get-tuple-element.27.au, f32[64,32,256]{2,1,0:T(8,128)S(1)} %get-tuple-element.28.av, f32[64,32,256]{2,1,0:T(8,128)S(1)} %advect_w.1.aw, ...), custom_call_target="tpu_custom_call" | custom-call | tf_op jit(solution)/shard_map/substeps/pallas_call | solution.py:441
  (23 shorter events, 0.0 us)
Async XLA Ops:
  0.6 1.0 copy-start
  1.7 1.0 copy-start.2
  2.7 1.0 copy-start.4
  3.8 1.0 copy-start.7
  4.8 0.7 copy-start.9
  5.5 47.3 %copy-start.1 = (f32[64,16,128]{2,1,0:T(8,128)S(1)}, f32[64,16,128]{2,1,0:T(8,128)}, u32[]{:S(2)}) copy-start(f32[64,16,128]{2,1,0:T(8,128)} %refs_0_.3) | copy-start | bytes 1572868
  5.5 47.3 %copy-start.3 = (f32[64,16,128]{2,1,0:T(8,128)S(1)}, f32[64,16,128]{2,1,0:T(8,128)}, u32[]{:S(2)}) copy-start(f32[64,16,128]{2,1,0:T(8,128)} %refs_0_.2) | copy-start | bytes 1572868
  5.5 47.3 %copy-start.11 = (f32[2,64]{1,0:T(2,128)S(1)}, f32[2,64]{1,0:T(2,128)}, u32[]{:S(2)}) copy-start(f32[2,64]{1,0:T(2,128)} %inflow.1) | copy-start | bytes 1540
  5.5 47.3 %copy-start.12 = (f32[64]{0:T(128)S(1)}, f32[64]{0:T(128)}, u32[]{:S(2)}) copy-start(f32[64]{0:T(128)} %stiff.1) | copy-start | bytes 772
  5.5 67.8 %copy-start.5 = (f32[64,16,128]{2,1,0:T(8,128)S(1)}, f32[64,16,128]{2,1,0:T(8,128)}, u32[]{:S(2)}) copy-start(f32[64,16,128]{2,1,0:T(8,128)} %u.5) | copy-start | bytes 1572868
  5.5 67.8 %copy-start.6 = (bf16[256,512]{1,0:T(8,128)(2,1)S(1)}, bf16[256,512]{1,0:T(8,128)(2,1)}, u32[]{:S(2)}) copy-start(bf16[256,512]{1,0:T(8,128)(2,1)} %constant.2.clone.band.refs_10_) | copy-start | bytes 786436
  5.5 67.8 %copy-start.8 = (f32[64,16,128]{2,1,0:T(8,128)S(1)}, f32[64,16,128]{2,1,0:T(8,128)}, u32[]{:S(2)}) copy-start(f32[64,16,128]{2,1,0:T(8,128)} %v.3) | copy-start | bytes 1572868
  5.5 67.8 %copy-start.10 = (s32[16,128]{1,0:T(8,128)S(1)}, s32[16,128]{1,0:T(8,128)}, u32[]{:S(2)}) copy-start(s32[16,128]{1,0:T(8,128)} %terrain.5) | copy-start | bytes 24580
  5.6 67.8 %copy-start.13 = (s32[4]{0:T(128)S(1)}, s32[4]{0:T(128)}, u32[]{:S(2)}) copy-start(s32[4]{0:T(128)} %zones.1) | copy-start | bytes 52
  7.1 60.4 %collective-permute-start.4 = (f32[128,8,128]{2,1,0:T(8,128)S(1)}, f32[128,8,128]{2,1,0:T(8,128)S(1)}, u32[]{:S(2)}, u32[]{:S(2)}) collective-permute-start(f32[128,8,128]{2,1,0:T(8,128)S(1)} %get-tuple-element.25), channel_id=1, source_target_pairs={{0,16},{16,32},{32,48},{48,64},{64,80},{80,96},{96,112},{1,17},{17... | collective-permute-start | bytes 1572872 | tf_op jit(solution)/shard_map/ppermute | solution.py:358
  12.0 32.9 %collective-permute-start = (f32[33,16,128]{2,1,0:T(8,128)S(1)}, f32[33,16,128]{2,1,0:T(8,128)S(1)}, u32[]{:S(2)}, u32[]{:S(2)}) collective-permute-start(f32[33,16,128]{2,1,0:T(8,128)S(1)} %get-tuple-element.21), channel_id=1, source_target_pairs={{1,0},{2,1},{3,2},{4,3},{5,4},{6,5},{7,6},{8,7},{9,8},{10,9},{11,1... | collective-permute-start | bytes 811016 | tf_op jit(solution)/shard_map/ppermute | solution.py:358
  14.8 30.0 %collective-permute-start.1 = (f32[33,16,128]{2,1,0:T(8,128)S(1)}, f32[33,16,128]{2,1,0:T(8,128)S(1)}, u32[]{:S(2)}, u32[]{:S(2)}) collective-permute-start(f32[33,16,128]{2,1,0:T(8,128)S(1)} %get-tuple-element.22), channel_id=1, source_target_pairs={{0,1},{1,2},{2,3},{3,4},{4,5},{5,6},{6,7},{7,8},{8,9},{9,10},{10,1... | collective-permute-start | bytes 811016 | tf_op jit(solution)/shard_map/ppermute | solution.py:358
  17.5 55.8 %collective-permute-start.5 = (f32[128,8,128]{2,1,0:T(8,128)S(1)}, f32[128,8,128]{2,1,0:T(8,128)S(1)}, u32[]{:S(2)}, u32[]{:S(2)}) collective-permute-start(f32[128,8,128]{2,1,0:T(8,128)S(1)} %get-tuple-element.26), channel_id=1, source_target_pairs={{16,0},{32,16},{48,32},{64,48},{80,64},{96,80},{112,96},{17,1},{33... | collective-permute-start | bytes 1572872 | tf_op jit(solution)/shard_map/ppermute | solution.py:358
  45.1 13.1 %collective-permute-start.2 = (f32[50,8,128]{2,1,0:T(8,128)S(1)}, f32[50,8,128]{2,1,0:T(8,128)S(1)}, u32[]{:S(2)}, u32[]{:S(2)}) collective-permute-start(f32[50,8,128]{2,1,0:T(8,128)S(1)} %get-tuple-element.23), channel_id=1, source_target_pairs={{0,16},{16,32},{32,48},{48,64},{64,80},{80,96},{96,112},{1,17},{17... | collective-permute-start | bytes 614408 | tf_op jit(solution)/shard_map/ppermute | solution.py:358
  47.0 18.6 %collective-permute-start.3 = (f32[50,8,128]{2,1,0:T(8,128)S(1)}, f32[50,8,128]{2,1,0:T(8,128)S(1)}, u32[]{:S(2)}, u32[]{:S(2)}) collective-permute-start(f32[50,8,128]{2,1,0:T(8,128)S(1)} %get-tuple-element.24), channel_id=1, source_target_pairs={{16,0},{32,16},{48,32},{64,48},{80,64},{96,80},{112,96},{17,1},{33... | collective-permute-start | bytes 614408 | tf_op jit(solution)/shard_map/ppermute | solution.py:358
  54.1 29.6 %collective-permute-start.8 = (f32[64,8,128]{2,1,0:T(8,128)S(1)}, f32[64,8,128]{2,1,0:T(8,128)S(1)}, u32[]{:S(2)}, u32[]{:S(2)}) collective-permute-start(f32[64,8,128]{2,1,0:T(8,128)S(1)} %get-tuple-element.34), channel_id=1, source_target_pairs={{0,16},{16,32},{32,48},{48,64},{64,80},{80,96},{96,112},{1,17},{17... | collective-permute-start | bytes 786440 | tf_op jit(solution)/shard_map/ppermute | solution.py:358
  58.2 25.4 %collective-permute-start.9 = (f32[64,8,128]{2,1,0:T(8,128)S(1)}, f32[64,8,128]{2,1,0:T(8,128)S(1)}, u32[]{:S(2)}, u32[]{:S(2)}) collective-permute-start(f32[64,8,128]{2,1,0:T(8,128)S(1)} %get-tuple-element.35), channel_id=1, source_target_pairs={{16,0},{32,16},{48,32},{64,48},{80,64},{96,80},{112,96},{17,1},{33... | collective-permute-start | bytes 786440 | tf_op jit(solution)/shard_map/ppermute | solution.py:358
  65.6 23.4 %collective-permute-start.6 = (f32[64,8,128]{2,1,0:T(8,128)S(1)}, f32[64,8,128]{2,1,0:T(8,128)S(1)}, u32[]{:S(2)}, u32[]{:S(2)}) collective-permute-start(f32[64,8,128]{2,1,0:T(8,128)S(1)} %get-tuple-element.32), channel_id=1, source_target_pairs={{0,16},{16,32},{32,48},{48,64},{64,80},{80,96},{96,112},{1,17},{17... | collective-permute-start | bytes 786440 | tf_op jit(solution)/shard_map/ppermute | solution.py:358
  67.6 21.5 %collective-permute-start.7 = (f32[64,8,128]{2,1,0:T(8,128)S(1)}, f32[64,8,128]{2,1,0:T(8,128)S(1)}, u32[]{:S(2)}, u32[]{:S(2)}) collective-permute-start(f32[64,8,128]{2,1,0:T(8,128)S(1)} %get-tuple-element.33), channel_id=1, source_target_pairs={{16,0},{32,16},{48,32},{64,48},{80,64},{96,80},{112,96},{17,1},{33... | collective-permute-start | bytes 786440 | tf_op jit(solution)/shard_map/ppermute | solution.py:358

commit v2 on v1

v2 whole, which is shorter than its diff:
```python
import functools

import jax
import jax.numpy as jnp
import numpy as np
from jax import lax
from jax.experimental import pallas as pl
from jax.experimental.pallas import tpu as pltpu
from jax.sharding import PartitionSpec as P

SUB = 6
ADV = 0.3
H = 0.4
RELAX = 0.5
WET_FROM = 8
HALO = 8

f32 = jnp.float32
UF, UD = 8, 8


def vmem():
    return pl.BlockSpec(memory_space=pltpu.VMEM)


def smem():
    return pl.BlockSpec(memory_space=pltpu.SMEM)


def lanes(shape):
    return lax.broadcasted_iota(jnp.int32, shape, len(shape) - 1)


def pack_a_kernel(u, v, w, p, terrain, ylo, yhi, west, east, *scratch):
    held, sems = scratch[0:4], scratch[4]
    nz = u.shape[0]
    groups = nz // 8
    half = nz // 2
    lane = lanes((16, 128))
    fields = (u, v, w, p)

    def copy(f, part):
        levels = pl.ds(part * half, half)
        return pltpu.make_async_copy(fields[f].at[levels], held[f].at[levels], sems.at[f, part])

    for f in range(4):
        for part in range(2):
            copy(f, part).start()
    solid = terrain[...].astype(f32)
    ylo[4 * groups] = solid
    yhi[4 * groups] = solid
    for f in range(4):
        for part in range(2):
            copy(f, part).wait()

            def body(t, carry, f=f, part=part):
                g = t + part * (groups // 2)
                rolled = []
                for s in range(8):
                    value = held[f][g * 8 + s]
                    rolled.append(pltpu.roll(value, 16 * s, 1))
                    if f < 2:
                        west[f * nz + g * 8 + s] = value[0:8]
                        east[f * nz + g * 8 + s] = value[8:16]
                low = rolled[0]
                high = rolled[0]
                for s in range(1, 8):
                    low = jnp.where(lane // 16 == s, rolled[s], low)
                    high = jnp.where(lane // 16 == s - 1, rolled[s], high)
                ylo[f * groups + g] = low
                yhi[f * groups + g] = high
                return carry

            lax.fori_loop(0, groups // 2, body, 0, unroll=2)


def pack_b_kernel(x, west, east):
    west[...] = x[:, 0:8, :]
    east[...] = x[:, 8:16, :]


def prepare_kernel(stiff, inflow, zones, coef, domain, *, block, nz):
    one = jnp.ones((8, 128), f32)
    above = jnp.zeros((8, 128), f32)
    ratio = jnp.zeros((8, 128), f32)
    for k in range(nz - 1, -1, -1):
        g = jnp.full((8, 128), stiff[k], f32)
        inverse = one / (one + g + above * (one - ratio))
        coef[0, k] = inverse
        coef[1, k] = above * inverse
        coef[2, k] = g * inverse
        coef[3, k] = g
        coef[4, k] = (H * H) * g
        coef[5, k] = jnp.full((8, 128), inflow[0, k], f32)
        coef[6, k] = jnp.full((8, 128), inflow[1, k], f32)
        ratio = g * inverse
        above = g
    shape = (32, 256)
    block_x, block_y = block
    total_x = block_x * lax.axis_size("gx")
    total_y = block_y * lax.axis_size("gy")
    row = lax.broadcasted_iota(jnp.int32, shape, 0) - HALO
    col = lanes(shape)
    col = jnp.where(col < 192, col, col - 256)
    at_x = lax.axis_index("gx") * block_x + row
    at_y = lax.axis_index("gy") * block_y + col
    inside = (at_x >= 0) & (at_x < total_x) & (at_y >= 0) & (at_y < total_y)
    inside = inside & (col < block_y + 16) & (col >= -16)
    inside = jnp.where(inside, 1.0, 0.0).astype(f32)
    at_x = at_x.astype(f32)
    at_y = at_y.astype(f32)
    ramp = jnp.zeros(shape, f32)
    for b, distance in enumerate((at_x, (total_x - 1.0) - at_x, at_y, (total_y - 1.0) - at_y)):
        width = jnp.full(shape, zones[b], jnp.int32).astype(f32)
        ramp = jnp.maximum(ramp, jnp.maximum(width - distance, 0.0) / width)
    relax = RELAX * ramp
    put(domain, 0, inside)
    put(domain, 1, jnp.where(inside > 0.0, 1.0 - relax, 0.0))
    put(domain, 2, jnp.where(inside > 0.0, relax, 0.0))


def put(ref, k, value, start=0):
    rows = slice(start, start + value.shape[0])
    ref[k, 0, rows, :] = value[:, 0:128]
    ref[k, 1, rows, :] = value[:, 128:256]


def both(ref, k, start=0, rows=32):
    at = slice(start, start + rows)
    return jnp.concatenate([ref[k, 0, at, :], ref[k, 1, at, :]], axis=1)


def pack_c_kernel(u, p, terrain, north, south, cw, ce):
    nz = u.shape[0]
    groups = nz // 8
    lane = lanes((16, 128))
    for t in range(4 * groups):
        corner = jnp.where(lane % 16 < 8, north[t], south[t])
        cw[t] = corner[0:8]
        ce[t] = corner[8:16]
    for f, ref in enumerate((u, p)):

        def body(g, carry, f=f, ref=ref):
            for s in range(8):
                cw[(4 + f) * groups + g, s : s + 1, :] = ref[g * 8 + s, 8:9, :]
                ce[(4 + f) * groups + g, s : s + 1, :] = ref[g * 8 + s, 7:8, :]
            return carry

        lax.fori_loop(0, groups, body, 0)
    solid = terrain[...].astype(f32)
    side = side_tile(lane, north[4 * groups], south[4 * groups])
    last = 6 * groups
    cw[last] = solid[0:8]
    ce[last] = solid[8:16]
    cw[last + 1] = side[0:8]
    ce[last + 1] = side[8:16]


def side_tile(lane, north, south):
    return jnp.where(lane < 16, north, jnp.where(lane >= 112, south, 0.0))


def packed_side(f, g, north, south, far_w, far_e, groups):
    t = f * groups + g
    lane = lanes((16, 128))
    own = jnp.where(lane % 16 < 8, north[t], south[t])
    return jnp.concatenate([far_w[t], own, far_e[t]], axis=0)


def extend(main, slot, ref, f, north, south, west, east, far_w, far_e, g, s, base=0):
    groups = ref.shape[0] // 8
    k = g * 8 + s
    lane16 = lanes((16, 128))
    lane8 = lanes((8, 128))
    back = (-16 * s) % 128
    t = f * groups + g
    own = side_tile(lane16, pltpu.roll(north[t], back, 1), pltpu.roll(south[t], back, 1))
    edge = (lane8 < 8) | (lane8 >= 120)
    corner_west = jnp.where(edge, pltpu.roll(far_w[t], back, 1), 0.0)
    corner_east = jnp.where(edge, pltpu.roll(far_e[t], back, 1), 0.0)
    value = jnp.concatenate([west[base + k], ref[k], east[base + k]], axis=0)
    main[slot, 8:40, :] = value
    if f in (0, 3):
        t = (4 if f == 0 else 5) * groups + g
        main[slot, 7:8, :] = far_w[t, s : s + 1, :]
        main[slot, 40:41, :] = far_e[t, s : s + 1, :]
    side = jnp.concatenate([corner_west, own, corner_east], axis=0)
    return value, side


BAND = ((0, 37, 10), (-1, 37, -10), (1, -8, -5), (-2, -8, 5), (2, 1, 1), (-3, 1, -1))


def band_matrix():
    band = np.zeros((256, 512), np.float32)
    j = np.arange(256)
    for by, centred, upwind in BAND:
        band[(j + by) % 256, j] = centred
        band[(j + by) % 256, 256 + j] = upwind
    return jnp.asarray(band, jnp.bfloat16)


def stage(parts, s, value):
    rows = slice(32 * s, 32 * s + 32)
    for part in parts:
        piece = value.astype(jnp.bfloat16)
        part[rows, :] = piece
        value = value - piece.astype(f32)


def along_sums(parts, band, sums):
    total = jnp.dot(parts[0][...], band[...], preferred_element_type=f32)
    for part in parts[1:]:
        total = total + jnp.dot(part[...], band[...], preferred_element_type=f32)
    sums[...] = total


def across_tendency(ref, slot, speed, flux_ref):
    def at(by):
        return ref[slot, 8 + by : 40 + by, :]

    value, before, after = at(0), at(-1), at(1)
    before2, after2 = at(-2), at(2)
    before3 = at(-3)
    centred = 37.0 * (value + before) - 8.0 * (after + before2) + (after2 + before3)
    upwind = 10.0 * (value - before) - 5.0 * (after - before2) + (after2 - before3)
    flux = speed * centred - jnp.abs(speed) * upwind
    flux_ref[slot, 0:32, :] = flux
    return flux_ref[slot, 1:33, :] - flux


def side_across(f, g, sources, groups, packed, flux_ref):
    speed = (ADV / 60.0) * packed_side(0, g, *sources, groups)
    packed[0, 8:40, :] = packed_side(f, g, *sources, groups)
    return across_tendency(packed, 0, speed, flux_ref)


def less_across(main, slot, side, speed, across, s, flux_ref):
    own = across_tendency(main, slot, (ADV / 60.0) * speed, flux_ref)
    across = jnp.concatenate([own, pltpu.roll(across, (-16 * s) % 128, 1)], axis=1)
    return jnp.concatenate([main[slot, 8:40, :], side], axis=1) - across


def along_tendency(v, sums, s):
    rows = slice(32 * s, 32 * s + 32)
    speed = (ADV / 60.0) * v
    flux = speed * sums[rows, 0:256] - jnp.abs(speed) * sums[rows, 256:512]
    return pltpu.roll(flux, 255, 1) - flux


def advect_uv_kernel(
    u,
    v,
    terrain,
    domain,
    north,
    south,
    cw,
    ce,
    west,
    east,
    band,
    xu,
    xv,
    au,
    av,
    masks,
    *scratch,
):
    parts, sums = (scratch[0:3], scratch[3:6]), scratch[6:8]
    vs, sides, packed, flux = scratch[8:12]
    nz = u.shape[0]
    groups = nz // 8
    lane = lanes((16, 128))
    own_side = side_tile(lane, north[4 * groups], south[4 * groups])
    last = 6 * groups
    solid = jnp.concatenate(
        [
            jnp.concatenate([cw[last], terrain[...].astype(f32), ce[last]], axis=0),
            jnp.concatenate([cw[last + 1], own_side, ce[last + 1]], axis=0),
        ],
        axis=1,
    )
    inside = both(domain, 0)
    for k in range(WET_FROM):
        put(masks, k, jnp.where(solid <= float(k), inside, 0.0))
    put(masks, WET_FROM, inside)

    def body(g, carry):
        sources = north, south, cw, ce
        arrived = (*sources[0:2], west, east, *sources[2:4])
        for s in range(8):
            k = g * 8 + s
            main, side = extend(xu, k, u, 0, *arrived, g, s)
            sides[s] = side
            stage(parts[0], s, jnp.concatenate([main, side], axis=1))
        along_sums(parts[0], band, sums[0])
        for s in range(8):
            main, side = extend(vs, s, v, 1, *arrived, g, s, nz)
            whole = jnp.concatenate([main, side], axis=1)
            put(xv, g * 8 + s, whole)
            stage(parts[1], s, whole)
        along_sums(parts[1], band, sums[1])
        for f in range(2):
            across = side_across(f, g, sources, groups, packed, flux)
            for s in range(8):
                k = g * 8 + s
                main, slot = ((xu, k), (vs, s))[f]
                side = sides[s] if f == 0 else xv[k, 1]
                rest = less_across(main, slot, side, xu[k, 8:40, :], across, s, flux)
                value = rest - along_tendency(both(xv, k), sums[f], s)
                put((au, av)[f], k, both(masks, jnp.minimum(k, WET_FROM)) * value)
        return carry

    lax.fori_loop(0, groups, body, 0)


def advect_one_kernel(
    x, xu, xv, masks, north, south, cw, ce, west, east, band, out, *scratch, f
):
    parts, sums = (scratch[0:3], scratch[3:6]), scratch[6:8]
    mains, sides, packed, flux = scratch[8:12]
    nz = x.shape[0]
    groups = nz // 8
    start = 8 if f == 3 else 0

    def body(t, carry):
        sources = north, south, cw, ce
        arrived = (*sources[0:2], west, east, *sources[2:4])
        for h in range(2):
            for s in range(8):
                main, side = extend(mains, 8 * h + s, x, f, *arrived, 2 * t + h, s)
                sides[8 * h + s] = side
                stage(parts[h], s, jnp.concatenate([main, side], axis=1))
            along_sums(parts[h], band, sums[h])
        for h in range(2):
            g = 2 * t + h
            across = side_across(f, g, sources, groups, packed, flux)
            for s in range(8):
                k, n = g * 8 + s, 8 * h + s
                rest = less_across(mains, n, sides[n], xu[k, 8:40, :], across, s, flux)
                value = rest - along_tendency(both(xv, k), sums[h], s)
                put(out, k, H * both(masks, jnp.minimum(k, WET_FROM)) * value, start)
        return carry

    lax.fori_loop(0, groups // 2, body, 0)


def advect_scratch(levels, fluxes):
    part = pltpu.VMEM((256, 256), jnp.bfloat16)
    shapes = ((levels, 48), (levels, 32), (1, 48), (fluxes, 40))
    held = [pltpu.VMEM((count, rows, 128), f32) for count, rows in shapes]
    return [part] * 6 + [pltpu.VMEM((256, 512), f32)] * 2 + held


def splat(tile, shape):
    tall = jnp.concatenate([tile] * (shape[0] // 8), axis=0)
    return jnp.concatenate([tall] * (shape[1] // 128), axis=1)


def substeps_kernel(
    au, av, aw, ap, masks, domain, coef, uo, vo, wo, po, us, vs, ws, ps, qs, ds
):
    nz = au.shape[0]

    for step in range(SUB):
        first, final = step == 0, step == SUB - 1
        ur, vr, wr, pr = (au, av, aw, ap) if first else (us, vs, ws, ps)

        def relaxed(value, keep, pull):
            return value if first else keep * value + pull

        def faces(k, masked):
            if final:
                keep, pull = domain[1, 0, 8:32, :], domain[2, 0, 8:32, :]
                keep_v, pull_v = both(domain, 1, 8, 16), both(domain, 2, 8, 16)
                if masked:
                    mask = both(masks, k, 8, 24)
                    pull, pull_v = mask[:, 0:128] * pull, mask[0:16] * pull_v
                u = relaxed(ur[k, 0, 8:32, :], keep, pull * splat(coef[5, k], (24, 128)))
                u = u - (pr[k, 0, 16:40, :] - pr[k, 0, 15:39, :])
                v = relaxed(both(vr, k, 8, 16), keep_v, pull_v * splat(coef[6, k], (16, 256)))
                p = both(pr, k, 16, 16)
                v = v - (p - pltpu.roll(p, 1, 1))
                if masked:
                    u, v = mask[:, 0:128] * u, mask[0:16] * v
                else:
                    u = jnp.concatenate([u[0:16], domain[0, 0, 24:32, :] * u[16:24]], axis=0)
                    far = domain[0, 1, 8:24, :] * v[:, 128:256]
                    v = jnp.concatenate([v[:, 0:128], far], axis=1)
                us[k, 0, 8:32, :] = u
                put(vs, k, v, 8)
                return
            keep, pull = both(domain, 1), both(domain, 2)
            p = both(pr, k, 8)
            if masked:
                mask = both(masks, k)
                pull = mask * pull
            u = relaxed(both(ur, k), keep, pull * splat(coef[5, k], p.shape))
            v = relaxed(both(vr, k), keep, pull * splat(coef[6, k], p.shape))
            u = u - (p - both(pr, k, 7))
            v = v - (p - pltpu.roll(p, 1, 1))
            if masked:
                u, v = mask * u, mask * v
            else:
                far = both(domain, 0, 24, 8) * u[24:32]
                u = jnp.concatenate([u[0:24], far], axis=0)
                far = domain[0, 1] * v[:, 128:256]
                v = jnp.concatenate([v[:, 0:128], far], axis=1)
            put(us, k, u)
            put(vs, k, v)

        def down(k, carry, masked):
            q_above, d_above = carry
            if final:
                u, u_east = us[k, 0, 8:24, :], us[k, 0, 9:25, :]
                v_all = both(vs, k, 8, 16)
                v, v_north = v_all[:, 0:128], pltpu.roll(v_all, 255, 1)[:, 0:128]
                p, w = pr[k, 0, 16:32, :], wr[k, 0, 8:24, :]
            else:
                u, u_east = both(us, k), both(us, k, 1)
                v = both(vs, k)
                v_north = pltpu.roll(v, 255, 1)
                p, w = both(pr, k, 8), both(wr, k)

            def level(n):
                return splat(coef[n, k], p.shape)

            divergence = (u_east - u) + (v_north - v)
            q = p - level(4) * divergence
            d = (w - (q_above - q)) * level(0) + level(1) * d_above
            if masked:
                mask = masks[k, 0, 8:24, :] if final else both(masks, k)
                d = mask * d
            if final:
                keep, pull = domain[1, 0, 8:24, :], domain[2, 0, 8:24, :]
                if masked:
                    pull = mask * pull
                uo[k] = keep * u + pull * level(5)
                vo[k] = keep * v + pull * level(6)
                qs[k, 0, 8:24, :] = q
                ds[k, 0, 8:24, :] = d
            else:
                put(qs, k, q)
                put(ds, k, d)
            return q, d

        def each_face(k, carry, masked):
            faces(k, masked)
            return carry

        lax.fori_loop(0, WET_FROM, lambda k, c: each_face(k, c, True), 0, unroll=UF)
        lax.fori_loop(WET_FROM, nz, lambda k, c: each_face(k, c, False), 0, unroll=28)
        zero = jnp.zeros((16, 128) if final else (32, 256), f32)
        carry = lax.fori_loop(
            0, nz - WET_FROM, lambda t, c: down(nz - 1 - t, c, False), (zero, zero), unroll=14
        )
        lax.fori_loop(
            0, WET_FROM, lambda t, c: down(WET_FROM - 1 - t, c, True), carry, unroll=UD
        )

        def up(k, below, masked):
            def level(n):
                return splat(coef[n, k], below.shape)

            if final:
                d, q = ds[k, 0, 8:24, :], qs[k, 0, 8:24, :]
                keep = domain[1, 0, 8:24, :]
            else:
                d, q, keep = both(ds, k), both(qs, k), both(domain, 1)
            w = d + level(2) * below
            p = q - level(3) * (w - below)
            if masked:
                p = (masks[k, 0, 8:24, :] if final else both(masks, k)) * p
            if final:
                wo[k] = (1.0 / H) * (keep * w)
                po[k] = (1.0 / H) * (keep * p)
            else:
                put(ws, k, keep * w)
                put(ps, k, keep * p, 8)
            return w

        below = lax.fori_loop(0, WET_FROM, lambda k, c: up(k, c, True), zero, unroll=8)
        lax.fori_loop(WET_FROM, nz, lambda k, c: up(k, c, False), below, unroll=8)


def neighbours(axis, by):
    size = lax.axis_size(axis)
    return [(i, i + by) for i in range(size) if 0 <= i + by < size]


def send(value, axis, by):
    return lax.ppermute(value, axis, neighbours(axis, by))


def on_device(u, v, w, p, terrain, zones, stiff, inflow):
    nz = u.shape[0]
    groups = nz // 8

    def room(mib):
        return pltpu.CompilerParams(vmem_limit_bytes=mib * 1024 * 1024)


    def arr(*shape):
        return jax.ShapeDtypeStruct(shape, f32)

    hbm = pl.BlockSpec(memory_space=pltpu.HBM)
    in_hbm = [pltpu.with_memory_space_constraint(x, pltpu.HBM) for x in (u, v, w, p)]
    ylo, yhi, uw, ue = pl.pallas_call(
        pack_a_kernel,
        out_shape=(arr(4 * groups + 1, 16, 128),) * 2 + (arr(2 * nz, 8, 128),) * 2,
        in_specs=[hbm] * 4 + [vmem()],
        out_specs=(vmem(),) * 4,
        scratch_shapes=[pltpu.VMEM((nz, 16, 128), f32)] * 4 + [pltpu.SemaphoreType.DMA((4, 2))],
        compiler_params=room(8),
        name="pack_a",
    )(*in_hbm, terrain)
    north = send(ylo, "gy", -1)
    south = send(yhi, "gy", 1)
    ue_in, uw_in = send(uw, "gx", -1), send(ue, "gx", 1)

    def slabs(x):
        return pl.pallas_call(
            pack_b_kernel,
            out_shape=(arr(nz, 8, 128),) * 2,
            in_specs=[vmem()],
            out_specs=(vmem(),) * 2,
            compiler_params=room(4),
        )(x)

    ww, we = slabs(w)
    we_in, ww_in = send(ww, "gx", -1), send(we, "gx", 1)
    pw, pe = slabs(p)
    pe_in, pw_in = send(pw, "gx", -1), send(pe, "gx", 1)
    cw, ce = pl.pallas_call(
        pack_c_kernel,
        out_shape=(arr(6 * groups + 2, 8, 128),) * 2,
        in_specs=[vmem()] * 5,
        out_specs=(vmem(),) * 2,
        compiler_params=room(4),
        name="pack_c",
    )(u, p, terrain, north, south)
    ce_in, cw_in = send(cw, "gx", -1), send(ce, "gx", 1)
    prepare = pl.pallas_call(
        functools.partial(prepare_kernel, block=u.shape[1:], nz=nz),
        out_shape=(arr(7, nz, 8, 128), arr(3, 2, 32, 128)),
        in_specs=[smem()] * 3,
        out_specs=(vmem(),) * 2,
        compiler_params=room(8),
        name="prepare",
    )
    coef, domain = prepare(stiff, inflow, zones)
    band = band_matrix()
    advect_uv = pl.pallas_call(
        advect_uv_kernel,
        out_shape=(arr(nz, 48, 128),)
        + (arr(nz, 2, 32, 128),) * 3
        + (arr(WET_FROM + 1, 2, 32, 128),),
        in_specs=[vmem()] * 11,
        out_specs=(vmem(),) * 5,
        scratch_shapes=advect_scratch(8, 64),
        compiler_params=room(20),
        name="advect_uv",
    )
    xu, xv, au, av, masks = advect_uv(
        u, v, terrain, domain, north, south, cw_in, ce_in, uw_in, ue_in, band
    )

    def advect_one(x, f, west, east):
        def kernel(*refs):
            advect_one_kernel(*refs, f=f)

        return pl.pallas_call(
            kernel,
            out_shape=arr(nz, 2, 40 if f == 3 else 32, 128),
            in_specs=[vmem()] * 11,
            out_specs=vmem(),
            scratch_shapes=advect_scratch(16, 16),
            compiler_params=room(16),
            name="advect_w" if f == 2 else "advect_p",
        )(x, xu, xv, masks, north, south, cw_in, ce_in, west, east, band)

    aw = advect_one(w, 2, ww_in, we_in)
    ap = advect_one(p, 3, pw_in, pe_in)
    out = arr(nz, 16, 128)
    return pl.pallas_call(
        substeps_kernel,
        out_shape=(out,) * 4,
        in_specs=[vmem()] * 7,
        out_specs=(vmem(),) * 4,
        scratch_shapes=[
            pltpu.VMEM((nz, 2, rows, 128), f32) for rows in (40, 32, 32, 40, 32, 32)
        ],
        compiler_params=room(34),
        name="substeps",
    )(au, av, aw, ap, masks, domain, coef)


def solution(mesh):
    field = P(None, "gx", "gy")
    return jax.shard_map(
        on_device,
        mesh=mesh,
        in_specs=(field, field, field, field, P("gx", "gy"), P(), P(), P()),
        out_specs=(field, field, field, field),
        check_vma=False,
    )
```

time: 114 us -> 105 us (0.921)
  the two profiles are of different devices: /device:TPU:99 before, /device:TPU:36 now
where the time goes in v2:
time: 105 us; the launch traced here: 104 us
  starting transfers between devices  35.6 us (34%)
  Pallas kernels  34.2 us (33%)
  waiting for transfers between devices  32.4 us (31%)
    ppermute x10, starting transfers between devices, send(): return lax.ppermute(value, axis, neighbours(axis, by))  35.6 us
    ppermute x10, waiting for transfers between devices, send(): return lax.ppermute(value, axis, neighbours(axis, by))  32.4 us
    pallas_call x1, Pallas kernels, on_device(): pl.pallas_call(substeps_kernel, out_shape=(out,) * 4, in_specs=[vmem()] *...  16.5 us
    pallas_call x2, Pallas kernels, advect_one(): pl.pallas_call(kernel, out_shape=arr(nz, 2, 40 if f == 3 else 32, 128), i...  6.88 us
    pallas_call x1, Pallas kernels, on_device(): advect_uv(u, v, terrain, domain, north, south, cw_in, ce_in, uw_in, ue_in...  6.72 us
    pallas_call x1, Pallas kernels, on_device(): pl.pallas_call(pack_a_kernel, out_shape=(arr(4 * groups + 1, 16, 128),) *...  2.64 us
  transfers between devices with their start and end apart: 10, of which 3 were waited for; matrix products, arithmetic and copies ran while one was open for 0% of the time, Pallas kernels for 11%

profile of v2, /device:TPU:36, one launch (start us, length us, event | category | flops | bytes accessed | tf_op | source)
XLA Modules:
  0.0 104.1 jit_solution(12232314203919423883)
XLA Ops:
  0.6 0.0 copy-start.3
  0.6 0.0 copy-start
  0.7 0.0 copy-start.1
  0.7 0.0 copy-start.2
  0.7 0.9 copy-done.5
  1.6 2.6 %pack_a.1 = (f32[33,16,128]{2,1,0:T(8,128)S(1)}, f32[33,16,128]{2,1,0:T(8,128)S(1)}, f32[128,8,128]{2,1,0:T(8,128)S(1)}, f32[128,8,128]{2,1,0:T(8,128)S(1)}) custom-call(f32[64,16,128]{2,1,0:T(8,128)} %u.5, f32[64,16,128]{2,1,0:T(8,128)} %v.3, f32[64,16,128]{2,1,0:T(8,128)} %refs_0_.2, f32[64,16,128]{2,1,0:T(8,128)} %refs_0_.3, s32[16,128]{1,0:T(8,128)S(1)} %copy-done.5), custom_call_target="tpu_custom_call" | custom-call | tf_op jit(solution)/shard_map/pack_a/pallas_call | solution.py:509
  4.3 5.1 %collective-permute-start.4 = (f32[128,8,128]{2,1,0:T(8,128)S(1)}, f32[128,8,128]{2,1,0:T(8,128)S(1)}, u32[]{:S(2)}, u32[]{:S(2)}) collective-permute-start(f32[128,8,128]{2,1,0:T(8,128)S(1)} %get-tuple-element.26), channel_id=1, source_target_pairs={{0,16},{16,32},{32,48},{48,64},{64,80},{80,96},{96,112},{1,17},{17... | collective-permute-start | bytes 1572872 | tf_op jit(solution)/shard_map/ppermute | solution.py:493
  9.4 1.9 %collective-permute-start = (f32[33,16,128]{2,1,0:T(8,128)S(1)}, f32[33,16,128]{2,1,0:T(8,128)S(1)}, u32[]{:S(2)}, u32[]{:S(2)}) collective-permute-start(f32[33,16,128]{2,1,0:T(8,128)S(1)} %get-tuple-element.22), channel_id=1, source_target_pairs={{1,0},{2,1},{3,2},{4,3},{5,4},{6,5},{7,6},{8,7},{9,8},{10,9},{11,1... | collective-permute-start | bytes 811016 | tf_op jit(solution)/shard_map/ppermute | solution.py:493
  11.3 2.4 %collective-permute-start.1 = (f32[33,16,128]{2,1,0:T(8,128)S(1)}, f32[33,16,128]{2,1,0:T(8,128)S(1)}, u32[]{:S(2)}, u32[]{:S(2)}) collective-permute-start(f32[33,16,128]{2,1,0:T(8,128)S(1)} %get-tuple-element.23), channel_id=1, source_target_pairs={{0,1},{1,2},{2,3},{3,4},{4,5},{5,6},{6,7},{7,8},{8,9},{9,10},{10,1... | collective-permute-start | bytes 811016 | tf_op jit(solution)/shard_map/ppermute | solution.py:493
  13.7 3.5 %collective-permute-start.5 = (f32[128,8,128]{2,1,0:T(8,128)S(1)}, f32[128,8,128]{2,1,0:T(8,128)S(1)}, u32[]{:S(2)}, u32[]{:S(2)}) collective-permute-start(f32[128,8,128]{2,1,0:T(8,128)S(1)} %get-tuple-element.27), channel_id=1, source_target_pairs={{16,0},{32,16},{48,32},{64,48},{80,64},{96,80},{112,96},{17,1},{33... | collective-permute-start | bytes 1572872 | tf_op jit(solution)/shard_map/ppermute | solution.py:493
  17.3 24.7 %collective-permute-done.north.refs_4_ = f32[33,16,128]{2,1,0:T(8,128)S(1)} collective-permute-done((f32[33,16,128]{2,1,0:T(8,128)S(1)}, f32[33,16,128]{2,1,0:T(8,128)S(1)}, u32[]{:S(2)}, u32[]{:S(2)}) %collective-permute-start) | collective-permute-done | bytes 270368 | tf_op jit(solution)/shard_map/ppermute | solution.py:493
  42.0 0.0 collective-permute-done.1.south.refs_5_
  42.0 0.2 pack_c.1
  42.2 1.9 %collective-permute-start.2 = (f32[50,8,128]{2,1,0:T(8,128)S(1)}, f32[50,8,128]{2,1,0:T(8,128)S(1)}, u32[]{:S(2)}, u32[]{:S(2)}) collective-permute-start(f32[50,8,128]{2,1,0:T(8,128)S(1)} %get-tuple-element.24), channel_id=1, source_target_pairs={{0,16},{16,32},{32,48},{48,64},{64,80},{80,96},{96,112},{1,17},{17... | collective-permute-start | bytes 614408 | tf_op jit(solution)/shard_map/ppermute | solution.py:493
  44.1 6.3 %collective-permute-start.3 = (f32[50,8,128]{2,1,0:T(8,128)S(1)}, f32[50,8,128]{2,1,0:T(8,128)S(1)}, u32[]{:S(2)}, u32[]{:S(2)}) collective-permute-start(f32[50,8,128]{2,1,0:T(8,128)S(1)} %get-tuple-element.25), channel_id=1, source_target_pairs={{16,0},{32,16},{48,32},{64,48},{80,64},{96,80},{112,96},{17,1},{33... | collective-permute-start | bytes 614408 | tf_op jit(solution)/shard_map/ppermute | solution.py:493
  50.5 1.9 %collective-permute-start.6 = (f32[64,8,128]{2,1,0:T(8,128)S(1)}, f32[64,8,128]{2,1,0:T(8,128)S(1)}, u32[]{:S(2)}, u32[]{:S(2)}) collective-permute-start(f32[64,8,128]{2,1,0:T(8,128)S(1)} %get-tuple-element.33), channel_id=1, source_target_pairs={{0,16},{16,32},{32,48},{48,64},{64,80},{80,96},{96,112},{1,17},{17... | collective-permute-start | bytes 786440 | tf_op jit(solution)/shard_map/ppermute | solution.py:493
  52.5 2.0 %collective-permute-done.2.cw.refs_6_ = f32[50,8,128]{2,1,0:T(8,128)S(1)} collective-permute-done((f32[50,8,128]{2,1,0:T(8,128)S(1)}, f32[50,8,128]{2,1,0:T(8,128)S(1)}, u32[]{:S(2)}, u32[]{:S(2)}) %collective-permute-start.2) | collective-permute-done | bytes 204832 | tf_op jit(solution)/shard_map/ppermute | solution.py:493
  54.5 4.3 %collective-permute-start.7 = (f32[64,8,128]{2,1,0:T(8,128)S(1)}, f32[64,8,128]{2,1,0:T(8,128)S(1)}, u32[]{:S(2)}, u32[]{:S(2)}) collective-permute-start(f32[64,8,128]{2,1,0:T(8,128)S(1)} %get-tuple-element.34), channel_id=1, source_target_pairs={{16,0},{32,16},{48,32},{64,48},{80,64},{96,80},{112,96},{17,1},{33... | collective-permute-start | bytes 786440 | tf_op jit(solution)/shard_map/ppermute | solution.py:493
  58.8 5.6 %collective-permute-done.3.ce.refs_7_ = f32[50,8,128]{2,1,0:T(8,128)S(1)} collective-permute-done((f32[50,8,128]{2,1,0:T(8,128)S(1)}, f32[50,8,128]{2,1,0:T(8,128)S(1)}, u32[]{:S(2)}, u32[]{:S(2)}) %collective-permute-start.3) | collective-permute-done | bytes 204832 | tf_op jit(solution)/shard_map/ppermute | solution.py:493
  64.4 1.9 %collective-permute-start.8 = (f32[64,8,128]{2,1,0:T(8,128)S(1)}, f32[64,8,128]{2,1,0:T(8,128)S(1)}, u32[]{:S(2)}, u32[]{:S(2)}) collective-permute-start(f32[64,8,128]{2,1,0:T(8,128)S(1)} %get-tuple-element.35), channel_id=1, source_target_pairs={{0,16},{16,32},{32,48},{48,64},{64,80},{80,96},{96,112},{1,17},{17... | collective-permute-start | bytes 786440 | tf_op jit(solution)/shard_map/ppermute | solution.py:493
  66.4 0.0 collective-permute-done.4.west
  66.4 6.3 %collective-permute-start.9 = (f32[64,8,128]{2,1,0:T(8,128)S(1)}, f32[64,8,128]{2,1,0:T(8,128)S(1)}, u32[]{:S(2)}, u32[]{:S(2)}) collective-permute-start(f32[64,8,128]{2,1,0:T(8,128)S(1)} %get-tuple-element.36), channel_id=1, source_target_pairs={{16,0},{32,16},{48,32},{64,48},{80,64},{96,80},{112,96},{17,1},{33... | collective-permute-start | bytes 786440 | tf_op jit(solution)/shard_map/ppermute | solution.py:493
  72.7 1.2 %prepare.1 = (f32[7,64,8,128]{3,2,1,0:T(8,128)S(1)}, f32[3,2,32,128]{3,2,1,0:T(8,128)S(1)}) custom-call(f32[64]{0:T(128)S(1)} %copy-done.8, f32[2,64]{1,0:T(2,128)S(1)} %copy-done.7, s32[4]{0:T(128)S(1)} %copy-done.9), custom_call_target="tpu_custom_call" | custom-call | tf_op jit(solution)/shard_map/prepare/pallas_call | solution.py:552
  73.9 0.0 collective-permute-done.5.east
  74.0 6.7 %advect_uv.1 = (f32[64,48,128]{2,1,0:T(8,128)S(1)}, f32[64,2,32,128]{3,2,1,0:T(8,128)S(1)}, f32[64,2,32,128]{3,2,1,0:T(8,128)S(1)}, f32[64,2,32,128]{3,2,1,0:T(8,128)S(1)}, f32[9,2,32,128]{3,2,1,0:T(8,128)S(1)}) custom-call(f32[64,16,128]{2,1,0:T(8,128)S(1)} %copy-done.2, f32[64,16,128]{2,1,0:T(8,128)S(1)} %copy-done.4, s32[16,128]{1,0:T(8,128)S(1)} %copy-done.6, ...), custom_call_target="tpu_custom_call" | custom-call | tf_op jit(solution)/shard_map/advect_uv/pallas_call | solution.py:565
  80.7 0.0 collective-permute-done.6.refs_8_
  80.7 0.0 collective-permute-done.7.refs_9_
  80.7 3.4 %advect_w.1.aw = f32[64,2,32,128]{3,2,1,0:T(8,128)S(1)} custom-call(f32[64,16,128]{2,1,0:T(8,128)S(1)} %copy-done.1, f32[64,48,128]{2,1,0:T(8,128)S(1)} %get-tuple-element.30.refs_1_, f32[64,2,32,128]{3,2,1,0:T(8,128)S(1)} %get-tuple-element.31.refs_2_, f32[9,2,32,128]{3,2,1,0:T(8,128)S(1)} %get-tuple-element.32.refs_3_.masks, ...), custom_call_target="tpu_custom_call" | custom-call | tf_op jit(solution)/shard_map/advect_w/pallas_call | solution.py:573
  84.2 0.0 collective-permute-done.8.refs_8_
  84.2 0.0 collective-permute-done.9.refs_9_
  84.2 3.4 %advect_p.1.ap = f32[64,2,40,128]{3,2,1,0:T(8,128)S(1)} custom-call(f32[64,16,128]{2,1,0:T(8,128)S(1)} %copy-done, f32[64,48,128]{2,1,0:T(8,128)S(1)} %get-tuple-element.30.refs_1_, f32[64,2,32,128]{3,2,1,0:T(8,128)S(1)} %get-tuple-element.31.refs_2_, f32[9,2,32,128]{3,2,1,0:T(8,128)S(1)} %get-tuple-element.32.refs_3_.masks, ...), custom_call_target="tpu_custom_call" | custom-call | tf_op jit(solution)/shard_map/advect_p/pallas_call | solution.py:573
  87.6 16.5 %substeps.1 = (f32[64,16,128]{2,1,0:T(8,128)}, f32[64,16,128]{2,1,0:T(8,128)}, f32[64,16,128]{2,1,0:T(8,128)}, f32[64,16,128]{2,1,0:T(8,128)}) custom-call(f32[64,2,32,128]{3,2,1,0:T(8,128)S(1)} %get-tuple-element.28.au, f32[64,2,32,128]{3,2,1,0:T(8,128)S(1)} %get-tuple-element.29.av, f32[64,2,32,128]{3,2,1,0:T(8,128)S(1)} %advect_w.1.aw, ...), custom_call_target="tpu_custom_call" | custom-call | tf_op jit(solution)/shard_map/substeps/pallas_call | solution.py:586
  (17 shorter events, 0.1 us)
Async XLA Ops:
  0.6 73.3 %copy-start.3 = (bf16[256,512]{1,0:T(8,128)(2,1)S(1)}, bf16[256,512]{1,0:T(8,128)(2,1)}, u32[]{:S(2)}) copy-start(bf16[256,512]{1,0:T(8,128)(2,1)} %constant.2.clone.band.refs_10_) | copy-start | bytes 786436
  0.6 41.3 %copy-start = (f32[64,16,128]{2,1,0:T(8,128)S(1)}, f32[64,16,128]{2,1,0:T(8,128)}, u32[]{:S(2)}) copy-start(f32[64,16,128]{2,1,0:T(8,128)} %refs_0_.3) | copy-start | bytes 1572868
  0.7 49.8 %copy-start.1 = (f32[64,16,128]{2,1,0:T(8,128)S(1)}, f32[64,16,128]{2,1,0:T(8,128)}, u32[]{:S(2)}) copy-start(f32[64,16,128]{2,1,0:T(8,128)} %refs_0_.2) | copy-start | bytes 1572868
  0.7 41.3 %copy-start.2 = (f32[64,16,128]{2,1,0:T(8,128)S(1)}, f32[64,16,128]{2,1,0:T(8,128)}, u32[]{:S(2)}) copy-start(f32[64,16,128]{2,1,0:T(8,128)} %u.5) | copy-start | bytes 1572868
  0.7 73.3 %copy-start.4 = (f32[64,16,128]{2,1,0:T(8,128)S(1)}, f32[64,16,128]{2,1,0:T(8,128)}, u32[]{:S(2)}) copy-start(f32[64,16,128]{2,1,0:T(8,128)} %v.3) | copy-start | bytes 1572868
  0.7 0.9 copy-start.5
  1.6 71.1 %copy-start.7 = (f32[2,64]{1,0:T(2,128)S(1)}, f32[2,64]{1,0:T(2,128)}, u32[]{:S(2)}) copy-start(f32[2,64]{1,0:T(2,128)} %inflow.1) | copy-start | bytes 1540
  1.6 71.1 %copy-start.8 = (f32[64]{0:T(128)S(1)}, f32[64]{0:T(128)}, u32[]{:S(2)}) copy-start(f32[64]{0:T(128)} %stiff.1) | copy-start | bytes 772
  1.6 71.1 %copy-start.9 = (s32[4]{0:T(128)S(1)}, s32[4]{0:T(128)}, u32[]{:S(2)}) copy-start(s32[4]{0:T(128)} %zones.1) | copy-start | bytes 52
  1.6 72.3 %copy-start.6 = (s32[16,128]{1,0:T(8,128)S(1)}, s32[16,128]{1,0:T(8,128)}, u32[]{:S(2)}) copy-start(s32[16,128]{1,0:T(8,128)} %terrain.5) | copy-start | bytes 24580
  4.3 62.1 %collective-permute-start.4 = (f32[128,8,128]{2,1,0:T(8,128)S(1)}, f32[128,8,128]{2,1,0:T(8,128)S(1)}, u32[]{:S(2)}, u32[]{:S(2)}) collective-permute-start(f32[128,8,128]{2,1,0:T(8,128)S(1)} %get-tuple-element.26), channel_id=1, source_target_pairs={{0,16},{16,32},{32,48},{48,64},{64,80},{80,96},{96,112},{1,17},{17... | collective-permute-start | bytes 1572872 | tf_op jit(solution)/shard_map/ppermute | solution.py:493
  9.4 32.6 %collective-permute-start = (f32[33,16,128]{2,1,0:T(8,128)S(1)}, f32[33,16,128]{2,1,0:T(8,128)S(1)}, u32[]{:S(2)}, u32[]{:S(2)}) collective-permute-start(f32[33,16,128]{2,1,0:T(8,128)S(1)} %get-tuple-element.22), channel_id=1, source_target_pairs={{1,0},{2,1},{3,2},{4,3},{5,4},{6,5},{7,6},{8,7},{9,8},{10,9},{11,1... | collective-permute-start | bytes 811016 | tf_op jit(solution)/shard_map/ppermute | solution.py:493
  11.3 30.7 %collective-permute-start.1 = (f32[33,16,128]{2,1,0:T(8,128)S(1)}, f32[33,16,128]{2,1,0:T(8,128)S(1)}, u32[]{:S(2)}, u32[]{:S(2)}) collective-permute-start(f32[33,16,128]{2,1,0:T(8,128)S(1)} %get-tuple-element.23), channel_id=1, source_target_pairs={{0,1},{1,2},{2,3},{3,4},{4,5},{5,6},{6,7},{7,8},{8,9},{9,10},{10,1... | collective-permute-start | bytes 811016 | tf_op jit(solution)/shard_map/ppermute | solution.py:493
  13.7 60.2 %collective-permute-start.5 = (f32[128,8,128]{2,1,0:T(8,128)S(1)}, f32[128,8,128]{2,1,0:T(8,128)S(1)}, u32[]{:S(2)}, u32[]{:S(2)}) collective-permute-start(f32[128,8,128]{2,1,0:T(8,128)S(1)} %get-tuple-element.27), channel_id=1, source_target_pairs={{16,0},{32,16},{48,32},{64,48},{80,64},{96,80},{112,96},{17,1},{33... | collective-permute-start | bytes 1572872 | tf_op jit(solution)/shard_map/ppermute | solution.py:493
  42.2 12.3 %collective-permute-start.2 = (f32[50,8,128]{2,1,0:T(8,128)S(1)}, f32[50,8,128]{2,1,0:T(8,128)S(1)}, u32[]{:S(2)}, u32[]{:S(2)}) collective-permute-start(f32[50,8,128]{2,1,0:T(8,128)S(1)} %get-tuple-element.24), channel_id=1, source_target_pairs={{0,16},{16,32},{32,48},{48,64},{64,80},{80,96},{96,112},{1,17},{17... | collective-permute-start | bytes 614408 | tf_op jit(solution)/shard_map/ppermute | solution.py:493
  44.1 20.3 %collective-permute-start.3 = (f32[50,8,128]{2,1,0:T(8,128)S(1)}, f32[50,8,128]{2,1,0:T(8,128)S(1)}, u32[]{:S(2)}, u32[]{:S(2)}) collective-permute-start(f32[50,8,128]{2,1,0:T(8,128)S(1)} %get-tuple-element.25), channel_id=1, source_target_pairs={{16,0},{32,16},{48,32},{64,48},{80,64},{96,80},{112,96},{17,1},{33... | collective-permute-start | bytes 614408 | tf_op jit(solution)/shard_map/ppermute | solution.py:493
  50.5 30.2 %collective-permute-start.6 = (f32[64,8,128]{2,1,0:T(8,128)S(1)}, f32[64,8,128]{2,1,0:T(8,128)S(1)}, u32[]{:S(2)}, u32[]{:S(2)}) collective-permute-start(f32[64,8,128]{2,1,0:T(8,128)S(1)} %get-tuple-element.33), channel_id=1, source_target_pairs={{0,16},{16,32},{32,48},{48,64},{64,80},{80,96},{96,112},{1,17},{17... | collective-permute-start | bytes 786440 | tf_op jit(solution)/shard_map/ppermute | solution.py:493
  54.5 26.2 %collective-permute-start.7 = (f32[64,8,128]{2,1,0:T(8,128)S(1)}, f32[64,8,128]{2,1,0:T(8,128)S(1)}, u32[]{:S(2)}, u32[]{:S(2)}) collective-permute-start(f32[64,8,128]{2,1,0:T(8,128)S(1)} %get-tuple-element.34), channel_id=1, source_target_pairs={{16,0},{32,16},{48,32},{64,48},{80,64},{96,80},{112,96},{17,1},{33... | collective-permute-start | bytes 786440 | tf_op jit(solution)/shard_map/ppermute | solution.py:493
  64.4 19.7 %collective-permute-start.8 = (f32[64,8,128]{2,1,0:T(8,128)S(1)}, f32[64,8,128]{2,1,0:T(8,128)S(1)}, u32[]{:S(2)}, u32[]{:S(2)}) collective-permute-start(f32[64,8,128]{2,1,0:T(8,128)S(1)} %get-tuple-element.35), channel_id=1, source_target_pairs={{0,16},{16,32},{32,48},{48,64},{64,80},{80,96},{96,112},{1,17},{17... | collective-permute-start | bytes 786440 | tf_op jit(solution)/shard_map/ppermute | solution.py:493
  66.4 17.8 %collective-permute-start.9 = (f32[64,8,128]{2,1,0:T(8,128)S(1)}, f32[64,8,128]{2,1,0:T(8,128)S(1)}, u32[]{:S(2)}, u32[]{:S(2)}) collective-permute-start(f32[64,8,128]{2,1,0:T(8,128)S(1)} %get-tuple-element.36), channel_id=1, source_target_pairs={{16,0},{32,16},{48,32},{64,48},{80,64},{96,80},{112,96},{17,1},{33... | collective-permute-start | bytes 786440 | tf_op jit(solution)/shard_map/ppermute | solution.py:493
